TPU v7x, 32 devices: a whole 2x2x4 slice. The times are simulated.
32 devices in a mesh: tp: 8 (over z, y), dp: 4 (over x, core).
Axes of the slice: x: 2, y: 2, z: 4, core: 2. Of those that a mesh axis runs over, the one named last changes fastest.
Arguments:
- normed: bfloat16 [1024, 4096], P(('dp', 'tp')), may hold values from -6 to 6
- cotangent: bfloat16 [1024, 8192], P('dp', 'tp'), may hold values from -1.5 to 1.5
- weight_tiles: bfloat16 [2, 2048, 128, 128], P(None, 'tp'), may hold values from -0.09375 to 0.09375
- slot_tile: int32 [2048], replicated, may hold values from 0 to 2047, as said below
Outputs:
- hidden: bfloat16 [1024, 8192], P('dp', 'tp')
- d_normed: bfloat16 [1024, 4096], P(('dp', 'tp'))
- grad_tiles: float32 [2, 2048, 128, 128], P(None, 'tp', 'dp')
Inputs may be any that keep to these rules, and one draw needn't show every extreme that they name: `slot_tile`: A permutation of 0 to 2047. Position p belongs to owner p // 256 at slot p % 256. Each owner holds 24 to 40 tiles of the tile columns t * 8 to (t + 1) * 8 - 1 of each index t of tp; in every draw some owner holds exactly 40 for some t.
All inputs are finite; a program needn't handle non-finite values.
Results may differ from a plain program's by a relative error of at most 0.018.
Values may be sent and summed in bfloat16 or wider, within the bound.
A program may use at most 128 MiB of HBM per device.

v0:
```python
import jax
import jax.numpy as jnp
from jax import lax
from jax.experimental import pallas as pl
from jax.experimental.pallas import tpu as pltpu
from jax.sharding import PartitionSpec as P


def index_tables(slot_tile, groups, me, owned_count, tile_rows, tile_cols, list_len):
    cols_dev = tile_cols // groups
    tiles = slot_tile.reshape(groups, owned_count)
    target = tiles % tile_cols // cols_dev
    before = jnp.arange(owned_count)[:, None] < jnp.arange(owned_count)[None, :]
    ranks = jnp.arange(list_len, dtype=jnp.int32)
    devices = jnp.arange(groups, dtype=jnp.int32)
    my_target = lax.dynamic_index_in_dim(target, me, 0, keepdims=False)
    same = (my_target[:, None] == my_target[None, :]) & before
    my_rank = jnp.sum(same.astype(jnp.int32), axis=0)
    my_key = my_target * list_len + my_rank
    keys = (devices[:, None] * list_len + ranks[None, :]).reshape(-1)
    slots = jnp.arange(owned_count, dtype=jnp.int32)
    send_slots = jnp.sum(jnp.where(keys[:, None] == my_key[None, :], slots[None, :], 0), axis=1)
    mine = target == me
    rank = jnp.dot(
        mine.astype(jnp.bfloat16), before.astype(jnp.bfloat16), preferred_element_type=jnp.float32
    ).astype(jnp.int32)
    place = devices[:, None] * list_len + rank
    local_ix = (tiles % tile_cols - me * cols_dev) * tile_rows + tiles // tile_cols
    local_ix = jnp.where(mine, local_ix, -1)
    flat_local = local_ix.reshape(-1)
    blocks = jnp.arange(owned_count, dtype=jnp.int32)
    from_place = jnp.sum(
        jnp.where(blocks[:, None] == flat_local[None, :], place.reshape(-1)[None, :], 0), axis=1
    )
    hit = mine[:, None, :] & (rank[:, None, :] == ranks[None, :, None])
    return_ix = jnp.sum(jnp.where(hit, local_ix[:, None, :], 0), axis=2).reshape(-1)
    return send_slots, my_key, from_place, return_ix


def take_tiles(source, indices):
    flat = source.reshape((-1,) + source.shape[-2:])
    return jnp.take(flat, indices.reshape(-1), axis=0, mode="clip")


def project_kernel(banded_ref, weights_ref, out_ref):
    pair = jnp.concatenate([weights_ref[0], weights_ref[1]], axis=1)
    out_ref[...] = jnp.dot(
        banded_ref[...], pair, preferred_element_type=jnp.float32
    ).astype(out_ref.dtype)


def project(banded, weights):
    tokens, depth = banded.shape
    blocks, _, tile = weights.shape
    chunk = min(tokens, 1024)
    return pl.pallas_call(
        project_kernel,
        grid=(tokens // chunk, blocks // 2),
        in_specs=[
            pl.BlockSpec((chunk, depth), lambda n, b: (n, 0)),
            pl.BlockSpec((2, depth, tile), lambda n, b: (b, 0, 0)),
        ],
        out_specs=pl.BlockSpec((chunk, 2 * tile), lambda n, b: (n, b)),
        out_shape=jax.ShapeDtypeStruct((tokens, blocks * tile), jnp.bfloat16),
        cost_estimate=pl.CostEstimate(
            flops=2 * tokens * depth * blocks * tile,
            bytes_accessed=2 * (tokens * depth + depth * blocks * tile + tokens * blocks * tile),
            transcendentals=0,
        ),
    )(banded, weights)


def outer_kernel(banded_t_ref, grads_ref, out_ref, total_ref):
    step = pl.program_id(1)
    tile = out_ref.shape[2]
    term = jnp.dot(banded_t_ref[...], grads_ref[...], preferred_element_type=jnp.float32)

    @pl.when(step == 0)
    def _():
        total_ref[...] = term

    @pl.when(step > 0)
    def _():
        total_ref[...] += term

    @pl.when(step == pl.num_programs(1) - 1)
    def _():
        for half in range(2):
            part = total_ref[:, half * tile : (half + 1) * tile]
            out_ref[half] = part.astype(out_ref.dtype)


def outer(banded_t, grads, tile):
    depth, tokens = banded_t.shape
    blocks = grads.shape[1] // tile
    chunk = min(tokens, 1024)
    return pl.pallas_call(
        outer_kernel,
        grid=(blocks // 2, tokens // chunk),
        in_specs=[
            pl.BlockSpec((depth, chunk), lambda b, n: (0, n)),
            pl.BlockSpec((chunk, 2 * tile), lambda b, n: (n, b)),
        ],
        out_specs=pl.BlockSpec((2, depth, tile), lambda b, n: (b, 0, 0)),
        out_shape=jax.ShapeDtypeStruct((blocks, depth, tile), jnp.bfloat16),
        scratch_shapes=[pltpu.VMEM((depth, 2 * tile), jnp.float32)],
        cost_estimate=pl.CostEstimate(
            flops=2 * tokens * depth * blocks * tile,
            bytes_accessed=2 * (tokens * depth + depth * blocks * tile + tokens * blocks * tile),
            transcendentals=0,
        ),
    )(banded_t, grads)


def local(normed, cotangent, weight_tiles, slot_tile):
    tp_size = lax.axis_size("tp")
    dp_size = lax.axis_size("dp")
    me_tp = lax.axis_index("tp")
    me_dp = lax.axis_index("dp")
    rows, width = normed.shape
    group_rows, cols = cotangent.shape
    owned_count, tile = weight_tiles.shape[1:3]
    tile_rows = width // tile
    cols_dev = cols // tile
    tile_cols = cols_dev * tp_size
    base_count = owned_count // tp_size
    list_len = base_count + base_count // 4
    band = tile // dp_size
    depth = tile_rows * band
    tokens = group_rows * dp_size
    send_slots, my_key, from_place, return_ix = index_tables(
        slot_tile, tp_size, me_tp, owned_count, tile_rows, tile_cols, list_len
    )

    by_band = normed.reshape(rows, tile_rows, dp_size, band).transpose(2, 0, 1, 3)
    by_band = by_band.reshape(dp_size, rows, depth)
    by_group = lax.all_to_all(by_band, "dp", split_axis=0, concat_axis=0, tiled=True)
    banded = lax.all_gather(by_group, "tp", axis=1, tiled=True).reshape(tokens, depth)

    travel = (tp_size, list_len, band, tile)
    own_rows = [
        lax.dynamic_slice(
            weight_tiles, (m, 0, me_dp * band, 0), (1, owned_count, band, tile)
        )
        for m in range(2)
    ]
    outgoing = [take_tiles(own_rows[m], send_slots).reshape(travel) for m in range(2)]
    weights, proj = [], []
    for m in range(2):
        with jax.named_scope(f"send{m}"):
            arrived = lax.all_to_all(outgoing[m], "tp", split_axis=0, concat_axis=0, tiled=True)
        with jax.named_scope(f"proj{m}"):
            weights.append(take_tiles(arrived, from_place).reshape(cols_dev, depth, tile))
            partial = project(banded, weights[m])
            proj.append(
                lax.psum_scatter(partial, "dp", scatter_dimension=0, tiled=True).astype(jnp.float32)
            )
    gate_proj, up_proj = proj
    sigmoid_gate = jax.nn.sigmoid(gate_proj)
    act_gate = gate_proj * sigmoid_gate
    hidden = (act_gate * up_proj).astype(jnp.bfloat16)
    cot_full = cotangent.astype(jnp.float32)
    grad_gate = (
        cot_full * up_proj * (sigmoid_gate * (1.0 + gate_proj * (1.0 - sigmoid_gate)))
    ).astype(jnp.bfloat16)
    grad_up = (cot_full * act_gate).astype(jnp.bfloat16)
    grads = [lax.all_gather(g, "dp", axis=0, tiled=True) for g in (grad_gate, grad_up)]
    banded_t = banded.T
    back = []
    for m in range(2):
        with jax.named_scope(f"outer{m}"):
            summed = outer(banded_t, grads[m], tile).reshape(owned_count, band, tile)
            back.append(take_tiles(summed, return_ix).reshape(travel))
    back[1], grads[0], grads[1] = lax.optimization_barrier((back[1], grads[0], grads[1]))
    result = []
    for m in range(2):
        with jax.named_scope(f"back{m}"):
            returned = lax.all_to_all(back[m], "tp", split_axis=0, concat_axis=0, tiled=True)
        result.append(take_tiles(returned, my_key).reshape(owned_count, band, tile))
    result = jnp.stack(result).astype(jnp.float32)

    with jax.named_scope("term"):
        term = sum(
            jnp.einsum(
                "nbj,bkj->nk",
                grads[m].reshape(tokens, cols_dev, tile),
                weights[m],
                preferred_element_type=jnp.float32,
            )
            for m in range(2)
        )
        term = term.astype(jnp.bfloat16).reshape(dp_size, tp_size, rows, depth)
        term = term.transpose(1, 0, 2, 3)
    d_band = lax.psum_scatter(term.reshape(-1, depth), "tp", scatter_dimension=0, tiled=True)
    d_band = d_band.reshape(dp_size, rows, depth)
    d_all = lax.all_gather(d_band, "dp", axis=0, tiled=False)
    d_rows = lax.dynamic_index_in_dim(d_all, me_dp, 1, keepdims=False)
    d_normed = d_rows.reshape(dp_size, rows, tile_rows, band).transpose(1, 2, 0, 3)
    return (hidden, d_normed.reshape(rows, width), result)


def solution(mesh):
    return jax.shard_map(
        local,
        mesh=mesh,
        in_specs=(P(("dp", "tp"), None), P("dp", "tp"), P(None, "tp", None, None), P()),
        out_specs=(P("dp", "tp"), P(("dp", "tp"), None), P(None, "tp", "dp", None)),
        check_vma=False,
    )
```

profile of v0, /device:TPU:0, one launch (start us, length us, event | category | flops | bytes accessed | tf_op | source)
XLA Modules:
  0.0 449.1 jit_solution(13937275515895610190)
XLA Ops:
  7.2 1.7 reshape.247
  8.9 0.2 copy.60
  9.1 1.8 reshape.248
  10.9 4.2 all-to-all-start
  15.5 0.2 select_reduce_fusion.2
  15.7 4.3 dynamic-slice_bitcast_fusion.1
  20.0 4.1 gather_fusion
  24.2 6.5 %all-to-all-start.1 = ((bf16[8,40,32,128]{3,2,1,0:T(8,128)(2,1)}), bf16[8,40,32,128]{3,2,1,0:T(8,128)(2,1)}, u32[]{:S(2)}, u32[]{:S(2)}) async-start(bf16[8,40,32,128]{3,2,1,0:T(8,128)(2,1)} %bitcast.75), calls=%async_computation.1 | async-start | bytes 5242880 | tf_op jit(solution)/shard_map/send0/all_to_all | solution.py:151
  30.7 0.9 copy.38
  31.7 0.1 convolution_convert_fusion
  31.9 3.0 gather_fusion.2
  34.9 81.3 %all-to-all-done.1 = bf16[8,40,32,128]{3,2,1,0:T(8,128)(2,1)} async-done(((bf16[8,40,32,128]{3,2,1,0:T(8,128)(2,1)}), bf16[8,40,32,128]{3,2,1,0:T(8,128)(2,1)}, u32[]{:S(2)}, u32[]{:S(2)}) %all-to-all-start.1) | async-done | bytes 2621472 | tf_op jit(solution)/shard_map/send0/all_to_all | solution.py:151
  116.2 3.6 all-to-all-start.2
  119.9 0.3 select_reduce_fusion
  120.2 5.7 %copy.39 = bf16[4,256,1024]{1,0,2:T(4,128)(2,1)} copy(bf16[4,256,1024]{2,0,1:T(4,128)(2,1)} %all-gather.5.cloned.1.call-done) | data formatting | bytes 4194304 | tf_op jit(solution)/shard_map/all_gather | solution.py:138
  125.9 3.4 copy.49
  129.3 4.0 copy.40.banded_ref
  133.3 3.9 gather_fusion.1
  137.3 6.0 %proj0.1 = bf16[1024,1024]{1,0:T(8,128)(2,1)} custom-call(bf16[1024,1024]{1,0:T(8,128)(2,1)} %copy.40.banded_ref, bf16[8,1024,128]{2,1,0:T(8,128)(2,1)} %bitcast.89), custom_call_target="tpu_custom_call" | custom-call | flops 2147483648 | bytes 6291456 | tf_op jit(solution)/shard_map/proj0/pallas_call | solution.py:56
  143.4 36.1 %all-to-all-done.2 = bf16[8,40,32,128]{3,2,1,0:T(8,128)(2,1)S(1)} async-done(((bf16[8,40,32,128]{3,2,1,0:T(8,128)(2,1)}), bf16[8,40,32,128]{3,2,1,0:T(8,128)(2,1)S(1)}, u32[]{:S(2)}, u32[]{:S(2)}) %all-to-all-start.2) | async-done | bytes 2621472 | tf_op jit(solution)/shard_map/send1/all_to_all | solution.py:151
  179.5 2.2 gather_fusion.3
  181.7 6.0 %proj1.1 = bf16[1024,1024]{1,0:T(8,128)(2,1)} custom-call(bf16[1024,1024]{1,0:T(8,128)(2,1)} %copy.40.banded_ref, bf16[8,1024,128]{2,1,0:T(8,128)(2,1)} %bitcast.91), custom_call_target="tpu_custom_call" | custom-call | flops 2147483648 | bytes 6291456 | tf_op jit(solution)/shard_map/proj1/pallas_call | solution.py:56
  187.8 30.4 %reduce-scatter.6.cloned.1.call-done = bf16[256,1024]{1,0:T(8,128)(2,1)} async-done(((bf16[1024,1024]{1,0:T(8,128)(2,1)}), bf16[256,1024]{1,0:T(8,128)(2,1)}) %reduce-scatter.6.cloned.1.call-update) | async-done | bytes 524304 | tf_op jit(solution)/shard_map/proj1/reduce_scatter | solution.py:156
  218.2 3.0 fusion.9
  221.2 0.5 all-gather.9.cloned.1.call-update
  221.8 0.2 select_reduce_fusion.1
  222.1 21.9 %all-gather.7.cloned.1.call-done.grads_ref = bf16[1024,1024]{1,0:T(8,128)(2,1)} async-done(((bf16[256,1024]{1,0:T(8,128)(2,1)}), bf16[1024,1024]{1,0:T(8,128)(2,1)}) %all-gather.7.cloned.1.call-update) | async-done | bytes 2097168 | tf_op jit(solution)/shard_map/all_gather | solution.py:167
  243.9 6.0 %outer1.1 = bf16[8,1024,128]{2,1,0:T(8,128)(2,1)} custom-call(bf16[1024,1024]{1,0:T(8,128)(2,1)} %bitcast.79, bf16[1024,1024]{1,0:T(8,128)(2,1)} %all-gather.7.cloned.1.call-done.grads_ref), custom_call_target="tpu_custom_call" | custom-call | flops 2147483648 | bytes 6291456 | tf_op jit(solution)/shard_map/outer1/pallas_call | solution.py:97
  250.0 4.2 gather_fusion.4
  254.2 13.8 %all-gather.9.cloned.1.call-done.grads_ref = bf16[1024,1024]{1,0:T(8,128)(2,1)} async-done(((bf16[256,1024]{1,0:T(8,128)(2,1)}), bf16[1024,1024]{1,0:T(8,128)(2,1)}) %all-gather.9.cloned.1.call-update) | async-done | bytes 2097168 | tf_op jit(solution)/shard_map/all_gather | solution.py:167
  267.9 5.5 %all-to-all-start.4 = ((bf16[8,40,32,128]{3,2,1,0:T(8,128)(2,1)}), bf16[8,40,32,128]{3,2,1,0:T(8,128)(2,1)S(1)}, u32[]{:S(2)}, u32[]{:S(2)}) async-start(bf16[8,40,32,128]{3,2,1,0:T(8,128)(2,1)} %bitcast.14), calls=%async_computation.7 | async-start | bytes 5242880 | tf_op jit(solution)/shard_map/back1/all_to_all | solution.py:178
  273.5 0.2 reduce-scatter.8.cloned.1.call-start
  273.7 4.7 %fusion.3 = f32[1024,1024,1]{1,0,2:T(8,128)S(1)} fusion(bf16[8,1024,128]{2,1,0:T(8,128)(2,1)} %bitcast.90, bf16[1024,1024]{1,0:T(8,128)(2,1)} %all-gather.9.cloned.1.call-done.grads_ref), kind=kOutput, calls=%fused_computation.13 | convolution fusion | flops 2147483648 | bytes 8388608 | tf_op jit(solution)/shard_map/term/nbj,bkj->nk/dot_general | solution.py:184
  278.5 2.4 fusion
  280.9 1.6 copy.44
  282.4 6.0 %outer0.1 = bf16[8,1024,128]{2,1,0:T(8,128)(2,1)} custom-call(bf16[1024,1024]{1,0:T(8,128)(2,1)} %bitcast.80, bf16[1024,1024]{1,0:T(8,128)(2,1)} %all-gather.9.cloned.1.call-done.grads_ref), custom_call_target="tpu_custom_call" | custom-call | flops 2147483648 | bytes 6291456 | tf_op jit(solution)/shard_map/outer0/pallas_call | solution.py:97
  288.5 4.2 gather_fusion.5
  292.7 57.6 %all-to-all-done.4 = bf16[8,40,32,128]{3,2,1,0:T(8,128)(2,1)S(1)} async-done(((bf16[8,40,32,128]{3,2,1,0:T(8,128)(2,1)}), bf16[8,40,32,128]{3,2,1,0:T(8,128)(2,1)S(1)}, u32[]{:S(2)}, u32[]{:S(2)}) %all-to-all-start.4) | async-done | bytes 2621472 | tf_op jit(solution)/shard_map/back1/all_to_all | solution.py:178
  350.2 4.4 all-to-all-start.3
  354.7 68.5 %reduce-scatter.8.cloned.1.call-done = bf16[128,1024]{1,0:T(8,128)(2,1)} async-done(((bf16[1024,1024]{1,0:T(8,128)(2,1)}), bf16[128,1024]{1,0:T(8,128)(2,1)}) %reduce-scatter.8.cloned.1.call-update) | async-done | bytes 262160 | tf_op jit(solution)/shard_map/reduce_scatter | solution.py:194
  423.3 2.2 gather_fusion.7
  425.5 4.1 gather_fusion.6
  429.6 5.5 %maximum_convert_fusion = f32[2,256,32,128]{3,2,1,0:T(8,128)} fusion(bf16[1,256,32,128]{3,2,1,0:T(8,128)(2,1)S(1)} %bitcast.82, bf16[1,256,32,128]{3,2,1,0:T(8,128)(2,1)} %bitcast.83), kind=kLoop, calls=%fused_computation.8 | loop fusion | flops 4194304 | bytes 12582912 | tf_op jit(solution)/shard_map/convert_element_type | solution.py:180
  435.1 2.7 all-gather.11.cloned.1.call-done
  437.9 1.0 constant_dynamic-slice_fusion
  438.8 0.8 reshape.265
  439.6 0.8 copy.46
  440.4 1.8 reshape.266
  (43 shorter events, 1.0 us)
Async XLA Ops:
  8.9 6.4 %copy-start.3 = (s32[2048]{0:T(1024)S(1)}, s32[2048]{0:T(1024)}, u32[]{:S(2)}) copy-start(s32[2048]{0:T(1024)} %param.7) | copy-start | bytes 24580
  10.9 13.3 %all-to-all-start = ((bf16[4,32,1024]{2,1,0:T(8,128)(2,1)}), bf16[4,32,1024]{2,1,0:T(8,128)(2,1)S(1)}, u32[]{:S(2)}, u32[]{:S(2)}) async-start(bf16[4,32,1024]{2,1,0:T(8,128)(2,1)} %reshape.248), calls=%async_computation | async-start | bytes 524288 | tf_op jit(solution)/shard_map/all_to_all | solution.py:137
  24.2 92.0 %all-to-all-start.1 = ((bf16[8,40,32,128]{3,2,1,0:T(8,128)(2,1)}), bf16[8,40,32,128]{3,2,1,0:T(8,128)(2,1)}, u32[]{:S(2)}, u32[]{:S(2)}) async-start(bf16[8,40,32,128]{3,2,1,0:T(8,128)(2,1)} %bitcast.75), calls=%async_computation.1 | async-start | bytes 5242880 | tf_op jit(solution)/shard_map/send0/all_to_all | solution.py:151
  30.7 89.5 %all-gather.5.cloned.1.call-start = ((), (), s32[]{:S(2)}) async-start(), calls=%async_computation.8 | async-start | bytes 2359296 | tf_op jit(solution)/shard_map/all_gather | solution.py:138
  116.2 63.3 %all-to-all-start.2 = ((bf16[8,40,32,128]{3,2,1,0:T(8,128)(2,1)}), bf16[8,40,32,128]{3,2,1,0:T(8,128)(2,1)S(1)}, u32[]{:S(2)}, u32[]{:S(2)}) async-start(bf16[8,40,32,128]{3,2,1,0:T(8,128)(2,1)} %bitcast.74), calls=%async_computation.3 | async-start | bytes 5242880 | tf_op jit(solution)/shard_map/send1/all_to_all | solution.py:151
  119.8 68.0 %reduce-scatter.4.cloned.1.call-start = ((), (), s32[]{:S(2)}) async-start(), calls=%async_computation.9 | async-start | bytes 2621440 | tf_op jit(solution)/shard_map/proj0/reduce_scatter | solution.py:156
  143.3 74.9 %reduce-scatter.6.cloned.1.call-start = ((), (), s32[]{:S(2)}) async-start(), calls=%async_computation.10 | async-start | bytes 2621440 | tf_op jit(solution)/shard_map/proj1/reduce_scatter | solution.py:156
  187.7 30.5 %copy-start.2 = (bf16[256,1024]{1,0:T(8,128)(2,1)S(1)}, bf16[256,1024]{1,0:T(8,128)(2,1)}, u32[]{:S(2)}) copy-start(bf16[256,1024]{1,0:T(8,128)(2,1)} %param.5) | copy-start | bytes 1572868
  187.7 56.2 %all-gather.7.cloned.1.call-start = ((), (), s32[]{:S(2)}) async-start(), calls=%async_computation.11 | async-start | bytes 2621440 | tf_op jit(solution)/shard_map/all_gather | solution.py:167
  221.2 46.8 %all-gather.9.cloned.1.call-start = ((), (), s32[]{:S(2)}) async-start(), calls=%async_computation.12 | async-start | bytes 2621440 | tf_op jit(solution)/shard_map/all_gather | solution.py:167
  267.9 82.3 %all-to-all-start.4 = ((bf16[8,40,32,128]{3,2,1,0:T(8,128)(2,1)}), bf16[8,40,32,128]{3,2,1,0:T(8,128)(2,1)S(1)}, u32[]{:S(2)}, u32[]{:S(2)}) async-start(bf16[8,40,32,128]{3,2,1,0:T(8,128)(2,1)} %bitcast.14), calls=%async_computation.7 | async-start | bytes 5242880 | tf_op jit(solution)/shard_map/back1/all_to_all | solution.py:178
  273.5 149.7 %reduce-scatter.8.cloned.1.call-start = ((), (), s32[]{:S(2)}) async-start(), calls=%async_computation.13 | async-start | bytes 2359296 | tf_op jit(solution)/shard_map/reduce_scatter | solution.py:194
  273.7 4.8 %copy-start.1 = (bf16[256,32,128]{2,1,0:T(8,128)(2,1)S(1)}, bf16[256,32,128]{2,1,0:T(8,128)(2,1)}, u32[]{:S(2)}) copy-start(bf16[256,32,128]{2,1,0:T(8,128)(2,1)} %gather_fusion.3) | copy-start | bytes 6291460
  273.7 4.8 %copy-start.4 = (bf16[1024,1024]{1,0:T(8,128)(2,1)S(1)}, bf16[1024,1024]{1,0:T(8,128)(2,1)}, u32[]{:S(2)}) copy-start(bf16[1024,1024]{1,0:T(8,128)(2,1)} %all-gather.7.cloned.1.call-done.grads_ref) | copy-start | bytes 6291460
  350.2 75.2 %all-to-all-start.3 = ((bf16[8,40,32,128]{3,2,1,0:T(8,128)(2,1)}), bf16[8,40,32,128]{3,2,1,0:T(8,128)(2,1)}, u32[]{:S(2)}, u32[]{:S(2)}) async-start(bf16[8,40,32,128]{3,2,1,0:T(8,128)(2,1)} %bitcast.24), calls=%async_computation.6 | async-start | bytes 5242880 | tf_op jit(solution)/shard_map/back0/all_to_all | solution.py:178
  354.6 83.2 %all-gather.11.cloned.1.call-start = ((), (), s32[]{:S(2)}) async-start(), calls=%async_computation.14 | async-start | bytes 1310720 | tf_op jit(solution)/shard_map/all_gather | solution.py:196
  425.4 4.1 copy-start
Sparse Core Ops, SparseCore 0:
  34.2 82.3 all-gather.4
  143.4 32.6 reduce-scatter.3
  187.8 30.3 reduce-scatter.5
  221.3 22.5 all-gather.6
  245.3 22.5 all-gather.8
  282.6 140.5 reduce-scatter.7
  424.8 13.0 all-gather.10
where the time goes:
time: 450 us; the launch traced here: 449 us
  waiting for transfers between devices  313 us (70%)
  local copies, waits for them, and re-layouts  56.1 us (12%)
  starting transfers between devices  24.7 us (5%)
  Pallas kernels  24.1 us (5%)
  between operations  14.3 us (3%)
  other arithmetic  9.59 us (2%)
  matrix products  7.27 us (2%)
    all_to_all x2, waiting for transfers between devices, local(): lax.all_to_all(outgoing[m], 'tp', split_axis=0, concat_axis=0, tiled=True)  117 us
    reduce_scatter x1, waiting for transfers between devices, local(): lax.psum_scatter(term.reshape(-1, depth), 'tp', scatter_dimension=0, tile...  68.5 us
    all_to_all x2, waiting for transfers between devices, local(): lax.all_to_all(back[m], 'tp', split_axis=0, concat_axis=0, tiled=True)  57.6 us
    all_gather x2, waiting for transfers between devices, local(): lax.all_gather(g, 'dp', axis=0, tiled=True)  35.6 us
    reduce_scatter x2, waiting for transfers between devices, local(): lax.psum_scatter(partial, 'dp', scatter_dimension=0, tiled=True)  30.4 us
    gather x8, local copies, waits for them, and re-layouts, take_tiles(): return jnp.take(flat, indices.reshape(-1), axis=0, mode='clip')  27.9 us
    pallas_call x2, Pallas kernels, outer(): pl.pallas_call(outer_kernel, grid=(blocks // 2, tokens // chunk), in_spec...  12.1 us
    pallas_call x2, Pallas kernels, project(): pl.pallas_call(project_kernel, grid=(tokens // chunk, blocks // 2), in_sp...  12 us
  transfers between devices with their start and end apart: 12, of which 8 were waited for; matrix products, arithmetic and copies ran while one was open for 14% of the time, Pallas kernels for 5%

commit v1 on v0

v1 whole, which is shorter than its diff:
```python
import functools

import jax
import jax.numpy as jnp
from jax import lax
from jax.experimental import pallas as pl
from jax.experimental.pallas import tpu as pltpu
from jax.sharding import PartitionSpec as P

MESH = pl.DeviceIdType.MESH
VMEM_LIMIT = 67_043_328
CORES = 2


def ring_width(n):
    width = 2
    while 4 * width * width <= n:
        width *= 2
    return width


def ring_pos(index, n):
    y_size = ring_width(n)
    z, y = lax.div(index, y_size), lax.rem(index, y_size)
    inner = lax.div(y + y_size - 1, y_size)
    odd = lax.rem(z, 2)
    snake = z * (y_size - 1) + (1 - odd) * (y - 1) + odd * (y_size - 1 - y)
    return inner * snake + (1 - inner) * (n - 1 - z)


def ring_index(pos, n):
    y_size = ring_width(n)
    z_size = n // y_size
    back = lax.div(pos, n - z_size)
    z = lax.div(pos, y_size - 1)
    k = lax.rem(pos, y_size - 1)
    odd = lax.rem(z, 2)
    y = (1 - odd) * (k + 1) + odd * (y_size - 1 - k)
    return (1 - back) * (z * y_size + y) + back * (n - 1 - pos) * y_size


class Ring:
    def __init__(self, n):
        self.n = n
        self.half = n // 2
        self.pos = ring_pos(lax.axis_index("tp"), n)

    def at(self, offset):
        return ring_index(lax.rem(self.pos + offset + self.n, self.n), self.n)


def hops(ring, way, piece):
    return ring.half if way == piece else ring.half - 1


def step_of(way):
    return 1 - 2 * way


def build_tables(slot_tile, me, owned, tile_rows, tile_cols, n, list_len):
    cols_dev = tile_cols // n
    mine = lax.dynamic_slice(slot_tile, (me * owned,), (owned,))
    row, col = mine // tile_cols, mine % tile_cols
    group = col // cols_dev
    local_col = col % cols_dev
    same = group[None, :] == group[:, None]
    places = jnp.arange(n * list_len, dtype=jnp.int32)
    slots = jnp.arange(owned, dtype=jnp.int32)

    def build(key, sub, n_sub):
        less = same & (key[None, :] < key[:, None])
        pos = jnp.sum(less.astype(jnp.int32), axis=1)
        place = group * list_len + pos
        hit = places[:, None] == place[None, :]

        def pick(value):
            return jnp.sum(jnp.where(hit, value[None, :], 0), axis=1)

        sub_at = pick(sub + 1)
        before = jnp.concatenate([jnp.zeros((1,), jnp.int32), sub_at[:-1]])
        keep = (sub_at == before) & (places % list_len > 0)
        buckets = jnp.arange(n * n_sub, dtype=jnp.int32)
        in_bucket = buckets[:, None] == (group * n_sub + sub)[None, :]
        last = jnp.max(jnp.where(in_bucket, pos[None, :] + 1, 0), axis=1)
        return pick(slots), pick(row), pick(local_col), keep.astype(jnp.int32), last, place

    by_col = build(col * tile_rows + row, local_col, cols_dev)
    by_row = build(row * tile_cols + col, row, tile_rows)
    return by_col, by_row


def forward_kernel(
    dims, slot_tab, row_tab, keep_tab, last_tab, x_ref, cot_ref, w_ref,
    hidden_ref, grads_ref, xt_ref,
    xg, ww, buf, part, send, recv, cot, load_sem, ag_send, ag_recv, rs_send, rs_recv,
):
    n, tile_rows, cols_dev, list_len, rows, tile, dp_size = dims
    ring = Ring(n)
    half = ring.half
    me = lax.axis_index("tp")
    piece_cols = cols_dev // 2
    piece_rows = tile_rows // 2

    own_rows = pl.ds(pl.multiple_of(me * rows, rows), rows)
    loads = [
        pltpu.make_async_copy(x_ref, xg.at[:, own_rows, :], load_sem.at[0]),
        pltpu.make_async_copy(w_ref.at[0], ww.at[:, :, pl.ds(0, tile)], load_sem.at[1]),
        pltpu.make_async_copy(w_ref.at[1], ww.at[:, :, pl.ds(tile, tile)], load_sem.at[2]),
        pltpu.make_async_copy(cot_ref, cot, load_sem.at[3]),
    ]
    for load in loads:
        load.start()

    barrier = pltpu.get_barrier_semaphore()
    for offset in (1, -1):
        pl.semaphore_signal(
            barrier, inc=1, device_id={"tp": ring.at(offset)}, device_id_type=MESH
        )
    pl.semaphore_wait(barrier, 2)
    loads[0].wait()

    def token_copy(way, piece, hop):
        shard = ring.at(-step_of(way) * hop)
        view = xg.at[
            pl.ds(piece * piece_rows, piece_rows),
            pl.ds(pl.multiple_of(shard * rows, rows), rows),
            :,
        ]
        return pltpu.make_async_remote_copy(
            src_ref=view, dst_ref=view,
            send_sem=ag_send.at[way, piece, hop], recv_sem=ag_recv.at[way, piece, hop],
            device_id={"tp": ring.at(step_of(way))}, device_id_type=MESH,
        )

    lanes = [(way, piece) for piece in range(2) for way in range(2)]
    for way, piece in lanes:
        token_copy(way, piece, 0).start()
    for hop in range(half):
        for way, piece in lanes:
            if hop < hops(ring, way, piece):
                token_copy(way, piece, hop).wait_recv()
                if hop + 1 < hops(ring, way, piece):
                    token_copy(way, piece, hop + 1).start()
    loads[1].wait()
    loads[2].wait()

    buf[0] = jnp.zeros(buf.shape[1:], buf.dtype)

    def compute(which, dest):
        def tile_step(j, carry):
            at = dest * list_len + j
            term = jnp.dot(
                xg[row_tab[at]], ww[slot_tab[at]], preferred_element_type=jnp.float32
            )
            buf[j + 1] = term + jnp.where(keep_tab[at] > 0, buf[j], 0.0)
            return carry

        lax.fori_loop(0, list_len, tile_step, 0)

        def column(c, carry):
            part[which, c] = buf[last_tab[dest * cols_dev + c]]
            return carry

        lax.fori_loop(0, cols_dev, column, 0)

    def sum_copy(way, piece, hop):
        return pltpu.make_async_remote_copy(
            src_ref=send.at[way, piece, hop], dst_ref=recv.at[way, piece, hop],
            send_sem=rs_send.at[way, piece, hop], recv_sem=rs_recv.at[way, piece, hop],
            device_id={"tp": ring.at(step_of(way))}, device_id_type=MESH,
        )

    def first_hop(way, piece):
        return half - hops(ring, way, piece)

    def push(which, way, piece, hop):
        fresh = hop == first_hop(way, piece)
        if not fresh:
            sum_copy(way, piece, hop - 1).wait_recv()

        def column(c, carry):
            value = part[which, piece * piece_cols + c]
            if not fresh:
                value = value + recv[way, piece, hop - 1, c].astype(jnp.float32)
            send[way, piece, hop, c] = value.astype(jnp.bfloat16)
            return carry

        lax.fori_loop(0, piece_cols, column, 0)
        sum_copy(way, piece, hop).start()

    compute(0, ring.at(half))
    push(0, 0, 0, 0)
    push(0, 1, 1, 0)

    for hop in range(1, half):
        compute(0, ring.at(half - hop))
        compute(1, ring.at(hop - half))
        push(0, 0, 1, hop)
        push(1, 1, 0, hop)
        push(0, 0, 0, hop)
        push(1, 1, 1, hop)

    compute(0, me)

    band = tile // dp_size
    parts = dp_size // CORES
    order = lax.broadcasted_iota(jnp.int32, (tile, tile), 0)
    source = lax.broadcasted_iota(jnp.int32, (tile, tile), 1)
    core = order // (parts * band)
    x_part = order // band % parts
    perm = (source == (x_part * CORES + core) * band + order % band).astype(jnp.bfloat16)

    def transpose_block(r, carry):
        turned = lax.dot_general(
            perm, xg[r], (((1,), (1,)), ((), ())), preferred_element_type=jnp.float32
        ).astype(jnp.bfloat16)
        for c in range(CORES):
            xt_ref[c, r] = turned[c * (tile // CORES) : (c + 1) * (tile // CORES)]
        return carry

    lax.fori_loop(0, tile_rows, transpose_block, 0)
    loads[3].wait()

    for piece in (1, 0):
        for way in range(2):
            sum_copy(way, piece, half - 1).wait_recv()
        for k in range(piece_cols):
            c = piece * piece_cols + k
            total = (
                part[0, c]
                + recv[0, piece, half - 1, k].astype(jnp.float32)
                + recv[1, piece, half - 1, k].astype(jnp.float32)
            )
            gate, up = total[:, :tile], total[:, tile:]
            s = jax.nn.sigmoid(gate)
            act = gate * s
            cotangent = cot[:, c * tile : (c + 1) * tile].astype(jnp.float32)
            hidden_ref[:, c * tile : (c + 1) * tile] = (act * up).astype(jnp.bfloat16)
            grads_ref[c, :, :tile] = (
                cotangent * up * (s * (1.0 + gate * (1.0 - s)))
            ).astype(jnp.bfloat16)
            grads_ref[c, :, tile:] = (cotangent * act).astype(jnp.bfloat16)

    for way, piece in lanes:
        for hop in range(hops(ring, way, piece)):
            token_copy(way, piece, hop).wait_send()
        for hop in range(first_hop(way, piece), half):
            sum_copy(way, piece, hop).wait_send()


def forward(tables, x, cotangent, weights, n, list_len, dp_size):
    slot_tab, row_tab, _, keep_tab, last_tab, _ = tables
    tile_rows, rows, tile = x.shape
    tokens, cols = cotangent.shape
    owned = weights.shape[1]
    cols_dev = cols // tile
    half = n // 2
    dims = (n, tile_rows, cols_dev, list_len, rows, tile, dp_size)
    smem = pl.BlockSpec(memory_space=pltpu.SMEM)
    hbm = pl.BlockSpec(memory_space=pl.ANY)
    vmem = pl.BlockSpec(memory_space=pltpu.VMEM)
    slots = (2, 2, half, cols_dev // 2, tokens, 2 * tile)
    return pl.pallas_call(
        functools.partial(forward_kernel, dims),
        name="forward",
        in_specs=[smem] * 4 + [hbm] * 3,
        out_specs=[vmem, vmem, vmem],
        out_shape=[
            jax.ShapeDtypeStruct((tokens, cols), jnp.bfloat16),
            jax.ShapeDtypeStruct((cols_dev, tokens, 2 * tile), jnp.bfloat16),
            jax.ShapeDtypeStruct((CORES, tile_rows, tile // CORES, tokens), jnp.bfloat16),
        ],
        scratch_shapes=[
            pltpu.VMEM((tile_rows, tokens, tile), jnp.bfloat16),
            pltpu.VMEM((owned, tile, 2 * tile), jnp.bfloat16),
            pltpu.VMEM((list_len + 1, tokens, 2 * tile), jnp.float32),
            pltpu.VMEM((2, cols_dev, tokens, 2 * tile), jnp.float32),
            pltpu.VMEM(slots, jnp.bfloat16),
            pltpu.VMEM(slots, jnp.bfloat16),
            pltpu.VMEM((tokens, cols), jnp.bfloat16),
            pltpu.SemaphoreType.DMA((4,)),
            pltpu.SemaphoreType.DMA((2, 2, half)),
            pltpu.SemaphoreType.DMA((2, 2, half)),
            pltpu.SemaphoreType.DMA((2, 2, half)),
            pltpu.SemaphoreType.DMA((2, 2, half)),
        ],
        compiler_params=pltpu.CompilerParams(
            collective_id=0, has_side_effects=True, vmem_limit_bytes=VMEM_LIMIT
        ),
    )(slot_tab, row_tab, keep_tab, last_tab, x, cotangent, weights)


def backward_kernel(
    dims, big, slot_tab, row_tab, col_tab, keep_tab, last_tab, grads_ref, xt_ref, w_ref,
    d_ref, parts_ref, *rest,
):
    n, tile_rows, cols_dev, list_len, rows, tokens, tile, dp_size = dims
    (gall, gw, ww, xt, buf, dx, stage, send, recv,
     load_sem, work_sem, g_send, g_recv, p_send, p_recv, t_sem,
     x_send, x_recv, x_local, rs_send, rs_recv) = rest
    ring = Ring(n)
    half = ring.half
    me = lax.axis_index("tp")
    me_dp = lax.axis_index("dp")
    core, x_part = lax.rem(me_dp, CORES), lax.div(me_dp, CORES)
    n_parts = dp_size // CORES
    band = tile // dp_size
    piece_cols = cols_dev // 2
    piece_rows = tile_rows // 2
    n_stage = stage.shape[0]
    partner = {"dp": x_part * CORES + 1 - core}

    own_cols = pl.ds(pl.multiple_of(me * cols_dev, cols_dev), cols_dev)
    loads = [
        pltpu.make_async_copy(grads_ref, gall.at[0, own_cols], load_sem.at[0]),
        pltpu.make_async_copy(xt_ref.at[core], xt.at[0], load_sem.at[1]),
        pltpu.make_async_copy(w_ref.at[0], ww.at[:, :, pl.ds(0, tile)], load_sem.at[2]),
        pltpu.make_async_copy(w_ref.at[1], ww.at[:, :, pl.ds(tile, tile)], load_sem.at[3]),
    ]
    for load in loads:
        load.start()

    barrier = pltpu.get_barrier_semaphore()
    for offset in (1, -1):
        pl.semaphore_signal(
            barrier, inc=1, device_id={"tp": ring.at(offset)}, device_id_type=MESH
        )
    pl.semaphore_signal(barrier, inc=1, device_id=partner, device_id_type=MESH)

    def x_device(off):
        return {"dp": lax.rem(x_part + off, n_parts) * CORES + core}

    for off in range(1, n_parts):
        pl.semaphore_signal(barrier, inc=1, device_id=x_device(off), device_id_type=MESH)
    pl.semaphore_wait(barrier, 3 + n_parts - 1)

    turned = pltpu.make_async_remote_copy(
        src_ref=xt_ref.at[1 - core], dst_ref=xt.at[1],
        send_sem=t_sem.at[0], recv_sem=t_sem.at[1],
        device_id=partner, device_id_type=MESH,
    )

    def piece_view(side, shard, piece):
        start = pl.multiple_of(shard * cols_dev + piece * piece_cols, piece_cols)
        return gall.at[side, pl.ds(start, piece_cols)]

    def grad_copy(way, piece, hop):
        view = piece_view(0, ring.at(-step_of(way) * hop), piece)
        return pltpu.make_async_remote_copy(
            src_ref=view, dst_ref=view,
            send_sem=g_send.at[way, piece, hop], recv_sem=g_recv.at[way, piece, hop],
            device_id={"tp": ring.at(step_of(way))}, device_id_type=MESH,
        )

    def group_number(offset):
        return offset % n

    def pair_copy(offset, piece):
        shard = ring.at(offset)
        g = group_number(offset)
        return pltpu.make_async_remote_copy(
            src_ref=piece_view(0, shard, piece), dst_ref=piece_view(1, shard, piece),
            send_sem=p_send.at[g, piece], recv_sem=p_recv.at[g, piece],
            device_id=partner, device_id_type=MESH,
        )

    def x_copy(i, offset, off):
        dest = lax.rem(x_part + off, n_parts)
        shard = ring.at(offset)
        return pltpu.make_async_remote_copy(
            src_ref=stage.at[i % n_stage, dest],
            dst_ref=parts_ref.at[
                x_part, pl.ds(pl.multiple_of(shard * list_len, list_len), list_len)
            ],
            send_sem=x_send.at[i, off - 1], recv_sem=x_recv.at[i, off - 1],
            device_id=x_device(off), device_id_type=MESH,
        )

    def keep_copy(i, offset):
        shard = ring.at(offset)
        return pltpu.make_async_copy(
            stage.at[i % n_stage, x_part],
            parts_ref.at[
                x_part, pl.ds(pl.multiple_of(shard * list_len, list_len), list_len)
            ],
            x_local.at[i],
        )

    def finish(i, offset):
        for off in range(1, n_parts):
            x_copy(i, offset, off).wait_send()
        keep_copy(i, offset).wait()

    lanes = [(0, 0), (1, 1), (0, 1), (1, 0)]
    loads[0].wait()
    for way, piece in lanes:
        grad_copy(way, piece, 0).start()
    for piece in range(2):
        pair_copy(0, piece).start()
    turned.start()

    dx[...] = jnp.zeros(dx.shape, dx.dtype)
    buf[0] = jnp.zeros(buf.shape[1:], buf.dtype)
    for load in loads[1:]:
        load.wait()
    turned.wait()

    done = []

    def process(offset):
        i = len(done)
        shard = ring.at(offset)
        for piece in range(2):
            pair_copy(offset, piece).wait_recv()
        cols = pl.ds(pl.multiple_of(shard * cols_dev, cols_dev), cols_dev)
        fills = [
            pltpu.make_async_copy(gall.at[side, cols], gw.at[side], work_sem.at[side])
            for side in range(2)
        ]
        for fill in fills:
            fill.start()
        if i >= n_stage:
            finish(i - n_stage, done[i - n_stage])
        for fill in fills:
            fill.wait()
        slot = i % n_stage

        def outer(j, carry):
            at = shard * list_len + j
            r, c = row_tab[at], col_tab[at]
            value = jnp.dot(
                xt[0, r], gw[0, c], preferred_element_type=jnp.float32
            ) + jnp.dot(xt[1, r], gw[1, c], preferred_element_type=jnp.float32)
            for k in range(n_parts):
                stage[slot, k, j] = value[k * band : (k + 1) * band].astype(jnp.bfloat16)
            return carry

        lax.fori_loop(0, list_len, outer, 0)
        for off in range(1, n_parts):
            x_copy(i, offset, off).start()
        keep_copy(i, offset).start()

        def back(j, carry):
            at = shard * list_len + j
            term = lax.dot_general(
                gw[0, col_tab[at]], ww[slot_tab[at]], (((1,), (1,)), ((), ())),
                preferred_element_type=jnp.float32,
            )
            buf[j + 1] = term + jnp.where(keep_tab[at] > 0, buf[j], 0.0)
            return carry

        lax.fori_loop(0, list_len, back, 0)

        def add_row(r, carry):
            dx[r] += buf[last_tab[shard * tile_rows + r]]
            return carry

        lax.fori_loop(0, tile_rows, add_row, 0)
        done.append(offset)

    def arrive(way, piece, hop):
        if hop >= hops(ring, way, piece):
            return
        grad_copy(way, piece, hop).wait_recv()
        if hop + 1 < hops(ring, way, piece):
            grad_copy(way, piece, hop + 1).start()
        pair_copy(-step_of(way) * (hop + 1), piece).start()

    process(0)
    for hop in range(half):
        arrive(0, 0, hop)
        arrive(1, 1, hop)
        if hop > 0:
            process(-hop)
        arrive(0, 1, hop)
        arrive(1, 0, hop)
        if hop > 0:
            process(hop)
    process(half)

    def sum_copy(way, piece, hop):
        return pltpu.make_async_remote_copy(
            src_ref=send.at[way, piece, hop], dst_ref=recv.at[way, piece, hop],
            send_sem=rs_send.at[way, piece, hop], recv_sem=rs_recv.at[way, piece, hop],
            device_id={"tp": ring.at(step_of(way))}, device_id_type=MESH,
        )

    def first_hop(way, piece):
        return half - hops(ring, way, piece)

    def own_term(dest, piece):
        return dx[
            pl.ds(piece * piece_rows, piece_rows),
            pl.ds(pl.multiple_of(dest * rows, rows), rows),
            :,
        ]

    def push(way, piece, hop):
        value = own_term(ring.at(step_of(way) * (half - hop)), piece)
        if hop > first_hop(way, piece):
            sum_copy(way, piece, hop - 1).wait_recv()
            value = value + recv[way, piece, hop - 1].astype(jnp.float32)
        send[way, piece, hop] = value.astype(jnp.bfloat16)
        sum_copy(way, piece, hop).start()

    push(0, 0, 0)
    push(1, 1, 0)
    for hop in range(1, half):
        for way, piece in ((0, 1), (1, 0), (0, 0), (1, 1)):
            push(way, piece, hop)
    for piece in range(2):
        for way in range(2):
            sum_copy(way, piece, half - 1).wait_recv()
        d_ref[pl.ds(piece * piece_rows, piece_rows)] = (
            own_term(me, piece)
            + recv[0, piece, half - 1].astype(jnp.float32)
            + recv[1, piece, half - 1].astype(jnp.float32)
        ).astype(jnp.bfloat16)

    for i in range(max(0, n - n_stage), n):
        finish(i, done[i])
    for i in range(n):
        for off in range(1, n_parts):
            x_copy(i, done[i], off).wait_recv()
    for way, piece in lanes:
        for hop in range(hops(ring, way, piece)):
            grad_copy(way, piece, hop).wait_send()
        for hop in range(first_hop(way, piece), half):
            sum_copy(way, piece, hop).wait_send()
    for offset in done:
        for piece in range(2):
            pair_copy(offset, piece).wait_send()


def backward(tables, grads, xt, weights, n, list_len, rows, dp_size):
    slot_tab, row_tab, col_tab, keep_tab, last_tab, _ = tables
    _, tile_rows, half_tile, tokens = xt.shape
    cols_dev, _, pair = grads.shape
    tile = pair // 2
    owned = weights.shape[1]
    half = n // 2
    band = tile // dp_size
    n_parts = dp_size // CORES
    n_stage = 4
    dims = (n, tile_rows, cols_dev, list_len, rows, tokens, tile, dp_size)
    smem = pl.BlockSpec(memory_space=pltpu.SMEM)
    hbm = pl.BlockSpec(memory_space=pl.ANY)
    vmem = pl.BlockSpec(memory_space=pltpu.VMEM)
    slots = (2, 2, half, tile_rows // 2, rows, tile)
    gall_shape = (2, n * cols_dev, tokens, pair)
    big = 2 * n * cols_dev * tokens * pair * 2 > 24 * 2**20
    sem = pltpu.SemaphoreType.DMA
    out_specs = [vmem, hbm]
    out_shape = [
        jax.ShapeDtypeStruct((tile_rows, rows, tile), jnp.bfloat16),
        jax.ShapeDtypeStruct((n_parts, n * list_len, band, pair), jnp.bfloat16),
    ]
    scratch = []
    if big:
        out_specs.append(hbm)
        out_shape.append(jax.ShapeDtypeStruct(gall_shape, jnp.bfloat16))
    else:
        scratch.append(pltpu.VMEM(gall_shape, jnp.bfloat16))
    scratch += [
        pltpu.VMEM((2, cols_dev, tokens, pair), jnp.bfloat16),
        pltpu.VMEM((owned, tile, pair), jnp.bfloat16),
        pltpu.VMEM((2, tile_rows, half_tile, tokens), jnp.bfloat16),
        pltpu.VMEM((list_len + 1, tokens, tile), jnp.float32),
        pltpu.VMEM((tile_rows, tokens, tile), jnp.float32),
        pltpu.VMEM((n_stage, n_parts, list_len, band, pair), jnp.bfloat16),
        pltpu.VMEM(slots, jnp.bfloat16),
        pltpu.VMEM(slots, jnp.bfloat16),
        sem((4,)), sem((2,)),
        sem((2, 2, half)), sem((2, 2, half)),
        sem((n, 2)), sem((n, 2)), sem((2,)),
        sem((n, n_parts - 1)), sem((n, n_parts - 1)), sem((n,)),
        sem((2, 2, half)), sem((2, 2, half)),
    ]
    results = pl.pallas_call(
        functools.partial(backward_kernel, dims, big),
        name="backward",
        in_specs=[smem] * 5 + [hbm] * 3,
        out_specs=out_specs,
        out_shape=out_shape,
        scratch_shapes=scratch,
        compiler_params=pltpu.CompilerParams(
            collective_id=1, has_side_effects=True, vmem_limit_bytes=VMEM_LIMIT
        ),
    )(slot_tab, row_tab, col_tab, keep_tab, last_tab, grads, xt, weights)
    return results[0], results[1]


def finish_kernel(place_ref, parts_ref, out_ref):
    n_parts = parts_ref.shape[0]
    _, chunk, _, tile = out_ref.shape
    base = pl.program_id(0) * chunk

    def one(p, carry):
        at = place_ref[base + p]
        total = parts_ref[0, at].astype(jnp.float32)
        for k in range(1, n_parts):
            total = total + parts_ref[k, at].astype(jnp.float32)
        out_ref[0, p] = total[:, :tile]
        out_ref[1, p] = total[:, tile:]
        return carry

    lax.fori_loop(0, chunk, one, 0)


def finish_sum(place, parts):
    owned = place.shape[0]
    n_parts, listed, band, pair = parts.shape
    tile = pair // 2
    steps = 8
    return pl.pallas_call(
        finish_kernel,
        name="finish",
        grid=(steps,),
        in_specs=[
            pl.BlockSpec(memory_space=pltpu.SMEM),
            pl.BlockSpec((n_parts, listed, band, pair), lambda i: (0, 0, 0, 0)),
        ],
        out_specs=pl.BlockSpec((2, owned // steps, band, tile), lambda i: (0, i, 0, 0)),
        out_shape=jax.ShapeDtypeStruct((2, owned, band, tile), jnp.float32),
        compiler_params=pltpu.CompilerParams(vmem_limit_bytes=VMEM_LIMIT),
    )(place, parts)


def local(normed, cotangent, weight_tiles, slot_tile):
    n = lax.axis_size("tp")
    dp_size = lax.axis_size("dp")
    me = lax.axis_index("tp")
    rows, width = normed.shape
    owned, tile = weight_tiles.shape[1:3]
    tile_rows = width // tile
    tile_cols = cotangent.shape[1] // tile * n
    base_count = owned // n
    list_len = base_count + base_count // 4
    by_col, by_row = build_tables(slot_tile, me, owned, tile_rows, tile_cols, n, list_len)
    x = normed.reshape(rows, tile_rows, tile).transpose(1, 0, 2)
    hidden, grads, xt = forward(by_col, x, cotangent, weight_tiles, n, list_len, dp_size)
    d, parts = backward(by_row, grads, xt, weight_tiles, n, list_len, rows, dp_size)
    grad_tiles = finish_sum(by_row[-1], parts)
    d_normed = d.transpose(1, 0, 2).reshape(rows, width)
    return hidden, d_normed, grad_tiles


def solution(mesh):
    return jax.shard_map(
        local,
        mesh=mesh,
        in_specs=(P(("dp", "tp"), None), P("dp", "tp"), P(None, "tp", None, None), P()),
        out_specs=(P("dp", "tp"), P(("dp", "tp"), None), P(None, "tp", "dp", None)),
        check_vma=False,
    )
```

time: 450 us -> 309 us (0.69)
  waiting for transfers between devices: 313 us -> 0 us
  Pallas kernels: 24.1 us -> 298 us
  local copies, waits for them, and re-layouts: 56.1 us -> 5.24 us
  starting transfers between devices: 24.7 us -> 0 us
  between operations: 14.3 us -> 0.68 us
  matrix products: 7.27 us -> 0 us
  other arithmetic: 9.59 us -> 4.23 us
    pallas_call x4 -> x3, Pallas kernels: 24.1 us -> 298 us  [the longest x1 168 us: backward(): pl.pallas_call(functools.partial(backward_kernel, dims, big), name='backw...]
    all_to_all x5 -> x0, waiting for transfers between devices: 175 us -> none  [the longest x2 117 us: local(): lax.all_to_all(outgoing[m], 'tp', split_axis=0, concat_axis=0, tiled=True)]
    reduce_scatter x3 -> x0, waiting for transfers between devices: 99 us -> none  [the longest x1 68.5 us: local(): lax.psum_scatter(term.reshape(-1, depth), 'tp', scatter_dimension=0, tile...]
    all_gather x4 -> x0, waiting for transfers between devices: 38.4 us -> none  [the longest x2 35.6 us: local(): lax.all_gather(g, 'dp', axis=0, tiled=True)]
    gather x8 -> x0, local copies, waits for them, and re-layouts: 27.9 us -> none  [take_tiles(): return jnp.take(flat, indices.reshape(-1), axis=0, mode='clip')]
    all_to_all x5 -> x0, starting transfers between devices: 24.3 us -> none  [the longest x2 10.1 us: local(): lax.all_to_all(outgoing[m], 'tp', split_axis=0, concat_axis=0, tiled=True)]
    reshape x9 -> x1, local copies, waits for them, and re-layouts: 16.2 us -> 1.67 us  [local(): d_normed = d.transpose(1, 0, 2).reshape(rows, width)]
    convert_element_type x2 -> x1, other arithmetic: 8.49 us -> 0.67 us  [build(): keep.astype(jnp.int32)]
  transfers between devices with their start and end apart: 12 -> 0, of which waited for: 8 -> 0; matrix products, arithmetic and copies ran while one was open for 14% -> 0% of each run, Pallas kernels for 5% -> 0%
where the time goes in v1:
time: 309 us; the launch traced here: 308 us
  Pallas kernels  298 us (96%)
  local copies, waits for them, and re-layouts  5.24 us (2%)
  other arithmetic  4.23 us (1%)
    pallas_call x1, Pallas kernels, backward(): pl.pallas_call(functools.partial(backward_kernel, dims, big), name='backw...  168 us
    pallas_call x1, Pallas kernels, forward(): pl.pallas_call(functools.partial(forward_kernel, dims), name='forward', i...  120 us
    pallas_call x1, Pallas kernels, finish_sum(): pl.pallas_call(finish_kernel, name='finish', grid=(steps,), in_specs=[pl....  9.62 us

profile of v1, /device:TPU:0, one launch (start us, length us, event | category | flops | bytes accessed | tf_op | source)
XLA Modules:
  0.0 308.2 jit_solution(1727517524741055647)
XLA Ops:
  0.6 0.8 multiply_add_fusion
  1.4 0.3 convert_reduce_fusion
  1.7 0.0 copy-start
  1.7 0.7 select_reduce_fusion.7.last_tab
  2.4 0.7 select_reduce_fusion.8.last_tab
  3.1 1.1 select_reduce_fusion
  4.2 0.7 and_convert_fusion
  4.9 0.0 copy-done
  4.9 1.7 bitcast_bitcast_fusion.x_ref
  6.6 120.2 %forward.1 = (bf16[256,1024]{1,0:T(8,128)(2,1)}, bf16[8,256,256]{2,1,0:T(8,128)(2,1)}, bf16[2,32,64,256]{3,2,1,0:T(8,128)(2,1)}) custom-call(s32[320]{0:T(512)} %get-tuple-element.18.slot_tab, s32[320]{0:T(512)} %get-tuple-element.16.row_tab, s32[320]{0:T(512)} %get-tuple-element.38.keep_tab, s32[64]{0:T(128)} %select_reduce_fusion.8.last_tab, ...), custom_call_target="tpu_custom_call" | custom-call | tf_op jit(solution)/shard_map/forward/pallas_call | solution.py:263
  126.8 168.2 %backward.1 = (bf16[32,32,128]{2,1,0:T(8,128)(2,1)}, bf16[2,320,32,256]{3,2,1,0:T(8,128)(2,1)}) custom-call(s32[320]{0:T(512)} %get-tuple-element.19.slot_tab, s32[320]{0:T(512)} %get-tuple-element.15.row_tab, s32[320]{0:T(512)} %get-tuple-element.14.col_tab, s32[320]{0:T(512)} %get-tuple-element.37.keep_tab, s32[256]{0:T(256)} %select_reduce_fusion.7.last_tab, ...), custom_call_target="tpu_custom_call" | custom-call | tf_op jit(solution)/shard_map/backward/pallas_call | solution.py:579
  295.0 1.7 copy_bitcast_fusion
  296.7 9.6 %finish.1 = f32[2,256,32,128]{3,2,1,0:T(8,128)} custom-call(s32[256]{0:T(256)} %copy-done, bf16[2,320,32,256]{3,2,1,0:T(8,128)(2,1)} %get-tuple-element.12.parts_ref), custom_call_target="tpu_custom_call" | custom-call | tf_op jit(solution)/shard_map/finish/pallas_call | solution.py:615
  306.3 1.9 copy.16
  (3 shorter events, 0.0 us)
Async XLA Ops:
  1.7 3.2 %copy-start = (s32[256]{0:T(256)}, s32[256]{0:T(256)S(1)}, u32[]{:S(2)}) copy-start(s32[256]{0:T(256)S(1)} %get-tuple-element.31.place_ref) | copy-start | bytes 3076

commit v2 on v1

--- a/solution.py
+++ b/solution.py
@@ -55,6 +55,17 @@
 
 def step_of(way):
     return 1 - 2 * way
+
+
+def unrolled(count, body):
+    by = 4 if count % 4 == 0 else 2 if count % 2 == 0 else 1
+
+    def steps(i, carry):
+        for u in range(by):
+            body(i * by + u)
+        return carry
+
+    lax.fori_loop(0, count // by, steps, 0)
 
 
 def build_tables(slot_tile, me, owned, tile_rows, tile_cols, n, list_len):
@@ -147,15 +158,14 @@
     buf[0] = jnp.zeros(buf.shape[1:], buf.dtype)
 
     def compute(which, dest):
-        def tile_step(j, carry):
+        def tile_step(j):
             at = dest * list_len + j
             term = jnp.dot(
                 xg[row_tab[at]], ww[slot_tab[at]], preferred_element_type=jnp.float32
             )
             buf[j + 1] = term + jnp.where(keep_tab[at] > 0, buf[j], 0.0)
-            return carry
-
-        lax.fori_loop(0, list_len, tile_step, 0)
+
+        unrolled(list_len, tile_step)
 
         def column(c, carry):
             part[which, c] = buf[last_tab[dest * cols_dev + c]]
@@ -401,20 +411,20 @@
 
     dx[...] = jnp.zeros(dx.shape, dx.dtype)
     buf[0] = jnp.zeros(buf.shape[1:], buf.dtype)
-    for load in loads[1:]:
-        load.wait()
+    loads[1].wait()
     turned.wait()
 
     done = []
-
-    def process(offset):
+    cells = {}
+
+    def weight_grads(offset, cell):
         i = len(done)
         shard = ring.at(offset)
         for piece in range(2):
             pair_copy(offset, piece).wait_recv()
         cols = pl.ds(pl.multiple_of(shard * cols_dev, cols_dev), cols_dev)
         fills = [
-            pltpu.make_async_copy(gall.at[side, cols], gw.at[side], work_sem.at[side])
+            pltpu.make_async_copy(gall.at[side, cols], gw.at[cell, side], work_sem.at[side])
             for side in range(2)
         ]
         for fill in fills:
@@ -425,38 +435,40 @@
             fill.wait()
         slot = i % n_stage
 
-        def outer(j, carry):
+        def outer(j):
             at = shard * list_len + j
             r, c = row_tab[at], col_tab[at]
             value = jnp.dot(
-                xt[0, r], gw[0, c], preferred_element_type=jnp.float32
-            ) + jnp.dot(xt[1, r], gw[1, c], preferred_element_type=jnp.float32)
+                xt[0, r], gw[cell, 0, c], preferred_element_type=jnp.float32
+            ) + jnp.dot(xt[1, r], gw[cell, 1, c], preferred_element_type=jnp.float32)
             for k in range(n_parts):
                 stage[slot, k, j] = value[k * band : (k + 1) * band].astype(jnp.bfloat16)
-            return carry
-
-        lax.fori_loop(0, list_len, outer, 0)
+
+        unrolled(list_len, outer)
         for off in range(1, n_parts):
             x_copy(i, offset, off).start()
         keep_copy(i, offset).start()
-
-        def back(j, carry):
+        done.append(offset)
+        cells[offset] = cell
+
+    def token_grads(offset):
+        shard = ring.at(offset)
+        cell = cells[offset]
+
+        def back(j):
             at = shard * list_len + j
             term = lax.dot_general(
-                gw[0, col_tab[at]], ww[slot_tab[at]], (((1,), (1,)), ((), ())),
+                gw[cell, 0, col_tab[at]], ww[slot_tab[at]], (((1,), (1,)), ((), ())),
                 preferred_element_type=jnp.float32,
             )
             buf[j + 1] = term + jnp.where(keep_tab[at] > 0, buf[j], 0.0)
-            return carry
-
-        lax.fori_loop(0, list_len, back, 0)
-
-        def add_row(r, carry):
+
+        unrolled(list_len, back)
+
+        def add_row(r):
             dx[r] += buf[last_tab[shard * tile_rows + r]]
-            return carry
-
-        lax.fori_loop(0, tile_rows, add_row, 0)
-        done.append(offset)
+
+        unrolled(tile_rows, add_row)
 
     def arrive(way, piece, hop):
         if hop >= hops(ring, way, piece):
@@ -466,17 +478,25 @@
             grad_copy(way, piece, hop + 1).start()
         pair_copy(-step_of(way) * (hop + 1), piece).start()
 
-    process(0)
+    weight_grads(0, 0)
+    loads[2].wait()
+    loads[3].wait()
+    token_grads(0)
     for hop in range(half):
         arrive(0, 0, hop)
         arrive(1, 1, hop)
+        if hop == half - 1:
+            weight_grads(half, 2)
         if hop > 0:
-            process(-hop)
-        arrive(0, 1, hop)
-        arrive(1, 0, hop)
-        if hop > 0:
-            process(hop)
-    process(half)
+            token_grads(-hop)
+            token_grads(hop)
+        if hop == half - 1:
+            token_grads(half)
+        else:
+            arrive(0, 1, hop)
+            arrive(1, 0, hop)
+            weight_grads(-hop - 1, 0)
+            weight_grads(hop + 1, 1)
 
     def sum_copy(way, piece, hop):
         return pltpu.make_async_remote_copy(
@@ -562,7 +582,7 @@
     else:
         scratch.append(pltpu.VMEM(gall_shape, jnp.bfloat16))
     scratch += [
-        pltpu.VMEM((2, cols_dev, tokens, pair), jnp.bfloat16),
+        pltpu.VMEM((3, 2, cols_dev, tokens, pair), jnp.bfloat16),
         pltpu.VMEM((owned, tile, pair), jnp.bfloat16),
         pltpu.VMEM((2, tile_rows, half_tile, tokens), jnp.bfloat16),
         pltpu.VMEM((list_len + 1, tokens, tile), jnp.float32),

time: 309 us -> 266 us (0.86)
  Pallas kernels: 298 us -> 256 us
    pallas_call x1, Pallas kernels: 168 us -> 133 us  [backward(): pl.pallas_call(functools.partial(backward_kernel, dims, big), name='backw...]
    pallas_call x1, Pallas kernels: 120 us -> 113 us  [forward(): pl.pallas_call(functools.partial(forward_kernel, dims), name='forward', i...]
where the time goes in v2:
time: 266 us
  Pallas kernels  256 us (96%)
  local copies, waits for them, and re-layouts  5.24 us (2%)
  other arithmetic  4.23 us (2%)
    pallas_call x1, Pallas kernels, backward(): pl.pallas_call(functools.partial(backward_kernel, dims, big), name='backw...  133 us
    pallas_call x1, Pallas kernels, forward(): pl.pallas_call(functools.partial(forward_kernel, dims), name='forward', i...  113 us
    pallas_call x1, Pallas kernels, finish_sum(): pl.pallas_call(finish_kernel, name='finish', grid=(steps,), in_specs=[pl....  9.62 us

profile of v2, /device:TPU:0, one launch (start us, length us, event | category | flops | bytes accessed | tf_op | source)
XLA Modules:
  0.0 266.1 jit_solution(4644820934258965149)
XLA Ops:
  0.6 0.8 multiply_add_fusion
  1.4 0.3 convert_reduce_fusion
  1.7 0.0 copy-start
  1.7 0.7 select_reduce_fusion.7.last_tab
  2.4 0.7 select_reduce_fusion.8.last_tab
  3.1 1.1 select_reduce_fusion
  4.2 0.7 and_convert_fusion
  4.9 0.0 copy-done
  4.9 1.7 bitcast_bitcast_fusion.x_ref
  6.6 112.9 %forward.1 = (bf16[256,1024]{1,0:T(8,128)(2,1)}, bf16[8,256,256]{2,1,0:T(8,128)(2,1)}, bf16[2,32,64,256]{3,2,1,0:T(8,128)(2,1)}) custom-call(s32[320]{0:T(512)} %get-tuple-element.18.slot_tab, s32[320]{0:T(512)} %get-tuple-element.16.row_tab, s32[320]{0:T(512)} %get-tuple-element.38.keep_tab, s32[64]{0:T(128)} %select_reduce_fusion.8.last_tab, ...), custom_call_target="tpu_custom_call" | custom-call | tf_op jit(solution)/shard_map/forward/pallas_call | solution.py:273
  119.5 133.5 %backward.1 = (bf16[32,32,128]{2,1,0:T(8,128)(2,1)}, bf16[2,320,32,256]{3,2,1,0:T(8,128)(2,1)}) custom-call(s32[320]{0:T(512)} %get-tuple-element.19.slot_tab, s32[320]{0:T(512)} %get-tuple-element.15.row_tab, s32[320]{0:T(512)} %get-tuple-element.14.col_tab, s32[320]{0:T(512)} %get-tuple-element.37.keep_tab, s32[256]{0:T(256)} %select_reduce_fusion.7.last_tab, ...), custom_call_target="tpu_custom_call" | custom-call | tf_op jit(solution)/shard_map/backward/pallas_call | solution.py:599
  253.0 1.7 copy_bitcast_fusion
  254.7 9.6 %finish.1 = f32[2,256,32,128]{3,2,1,0:T(8,128)} custom-call(s32[256]{0:T(256)} %copy-done, bf16[2,320,32,256]{3,2,1,0:T(8,128)(2,1)} %get-tuple-element.12.parts_ref), custom_call_target="tpu_custom_call" | custom-call | tf_op jit(solution)/shard_map/finish/pallas_call | solution.py:635
  264.3 1.9 copy.16
  (3 shorter events, 0.0 us)
Async XLA Ops:
  1.7 3.2 %copy-start = (s32[256]{0:T(256)}, s32[256]{0:T(256)S(1)}, u32[]{:S(2)}) copy-start(s32[256]{0:T(256)S(1)} %get-tuple-element.31.place_ref) | copy-start | bytes 3076

commit v3 on v2

--- a/solution.py
+++ b/solution.py
@@ -21,9 +21,9 @@
 
 def ring_pos(index, n):
     y_size = ring_width(n)
-    z, y = lax.div(index, y_size), lax.rem(index, y_size)
-    inner = lax.div(y + y_size - 1, y_size)
-    odd = lax.rem(z, 2)
+    z, y = index // y_size, index % y_size
+    inner = (y + y_size - 1) // y_size
+    odd = z % 2
     snake = z * (y_size - 1) + (1 - odd) * (y - 1) + odd * (y_size - 1 - y)
     return inner * snake + (1 - inner) * (n - 1 - z)
 
@@ -39,6 +39,29 @@
     return (1 - back) * (z * y_size + y) + back * (n - 1 - pos) * y_size
 
 
+def arrival(index, me, n):
+    offset = (ring_pos(index, n) - ring_pos(me, n) + n) % n
+    behind = 2 * (n - offset) - 1
+    return jnp.where(offset == 0, 0, jnp.where(offset < n // 2, 2 * offset, behind))
+
+
+def arrival_plan(n, owned):
+    base = owned // n
+    low, high = base - base // 4, base + base // 4
+    chunks, cells, start = [], 4, 0
+    for step in range(n // 2 + 1):
+        landed = min(2 * step + 1, n)
+        stop = max(low * landed, owned - high * (n - landed))
+        cells = max(cells, landed - start // high)
+        if stop - start > high:
+            middle = start + (stop - start) // 4 * 2
+            chunks += [(step, start, middle - start), (step, middle, stop - middle)]
+        else:
+            chunks.append((step, start, stop - start))
+        start = stop
+    return chunks, cells
+
+
 class Ring:
     def __init__(self, n):
         self.n = n
@@ -97,13 +120,24 @@
 
     by_col = build(col * tile_rows + row, local_col, cols_dev)
     by_row = build(row * tile_cols + col, row, tile_rows)
-    return by_col, by_row
+
+    order = arrival(group, me, n)
+    key = order * owned + slots
+    rank = jnp.sum((key[None, :] < key[:, None]).astype(jnp.int32), axis=1)
+    _, cells = arrival_plan(n, owned)
+    block = order % cells * cols_dev + local_col
+    hit = slots[:, None] == rank[None, :]
+
+    def pick(value):
+        return jnp.sum(jnp.where(hit, value[None, :], 0), axis=1)
+
+    return by_col, by_row, (pick(row), pick(block), rank)
 
 
 def forward_kernel(
     dims, slot_tab, row_tab, keep_tab, last_tab, x_ref, cot_ref, w_ref,
     hidden_ref, grads_ref, xt_ref,
-    xg, ww, buf, part, send, recv, cot, load_sem, ag_send, ag_recv, rs_send, rs_recv,
+    xg, ww, buf, part, send, recv, cot, x_sem, load_sem, ag_send, ag_recv, rs_send, rs_recv,
 ):
     n, tile_rows, cols_dev, list_len, rows, tile, dp_size = dims
     ring = Ring(n)
@@ -114,12 +148,17 @@
 
     own_rows = pl.ds(pl.multiple_of(me * rows, rows), rows)
     loads = [
-        pltpu.make_async_copy(x_ref, xg.at[:, own_rows, :], load_sem.at[0]),
+        pltpu.make_async_copy(cot_ref, cot, load_sem.at[3]),
         pltpu.make_async_copy(w_ref.at[0], ww.at[:, :, pl.ds(0, tile)], load_sem.at[1]),
         pltpu.make_async_copy(w_ref.at[1], ww.at[:, :, pl.ds(tile, tile)], load_sem.at[2]),
-        pltpu.make_async_copy(cot_ref, cot, load_sem.at[3]),
     ]
-    for load in loads:
+    own = [
+        pltpu.make_async_copy(
+            x_ref.at[:, pl.ds(r * tile, tile)], xg.at[r, own_rows, :], x_sem.at[r]
+        )
+        for r in range(tile_rows)
+    ]
+    for load in own + loads:
         load.start()
 
     barrier = pltpu.get_barrier_semaphore()
@@ -128,7 +167,8 @@
             barrier, inc=1, device_id={"tp": ring.at(offset)}, device_id_type=MESH
         )
     pl.semaphore_wait(barrier, 2)
-    loads[0].wait()
+    for load in own:
+        load.wait()
 
     def token_copy(way, piece, hop):
         shard = ring.at(-step_of(way) * hop)
@@ -229,7 +269,7 @@
         return carry
 
     lax.fori_loop(0, tile_rows, transpose_block, 0)
-    loads[3].wait()
+    loads[0].wait()
 
     for piece in (1, 0):
         for way in range(2):
@@ -260,7 +300,9 @@
 
 def forward(tables, x, cotangent, weights, n, list_len, dp_size):
     slot_tab, row_tab, _, keep_tab, last_tab, _ = tables
-    tile_rows, rows, tile = x.shape
+    rows, width = x.shape
+    tile = weights.shape[2]
+    tile_rows = width // tile
     tokens, cols = cotangent.shape
     owned = weights.shape[1]
     cols_dev = cols // tile
@@ -288,6 +330,7 @@
             pltpu.VMEM(slots, jnp.bfloat16),
             pltpu.VMEM(slots, jnp.bfloat16),
             pltpu.VMEM((tokens, cols), jnp.bfloat16),
+            pltpu.SemaphoreType.DMA((tile_rows,)),
             pltpu.SemaphoreType.DMA((4,)),
             pltpu.SemaphoreType.DMA((2, 2, half)),
             pltpu.SemaphoreType.DMA((2, 2, half)),
@@ -301,7 +344,7 @@
 
 
 def backward_kernel(
-    dims, big, slot_tab, row_tab, col_tab, keep_tab, last_tab, grads_ref, xt_ref, w_ref,
+    dims, plan, slot_tab, col_tab, keep_tab, last_tab, list_row, list_block, grads_ref, xt_ref, w_ref,
     d_ref, parts_ref, *rest,
 ):
     n, tile_rows, cols_dev, list_len, rows, tokens, tile, dp_size = dims
@@ -318,6 +361,7 @@
     piece_cols = cols_dev // 2
     piece_rows = tile_rows // 2
     n_stage = stage.shape[0]
+    chunks, cells = plan
     partner = {"dp": x_part * CORES + 1 - core}
 
     own_cols = pl.ds(pl.multiple_of(me * cols_dev, cols_dev), cols_dev)
@@ -374,32 +418,28 @@
             device_id=partner, device_id_type=MESH,
         )
 
-    def x_copy(i, offset, off):
+    def x_copy(i, off):
+        _, start, size = chunks[i]
         dest = lax.rem(x_part + off, n_parts)
-        shard = ring.at(offset)
         return pltpu.make_async_remote_copy(
-            src_ref=stage.at[i % n_stage, dest],
-            dst_ref=parts_ref.at[
-                x_part, pl.ds(pl.multiple_of(shard * list_len, list_len), list_len)
-            ],
+            src_ref=stage.at[i % n_stage, dest, pl.ds(0, size)],
+            dst_ref=parts_ref.at[x_part, pl.ds(start, size)],
             send_sem=x_send.at[i, off - 1], recv_sem=x_recv.at[i, off - 1],
             device_id=x_device(off), device_id_type=MESH,
         )
 
-    def keep_copy(i, offset):
-        shard = ring.at(offset)
+    def keep_copy(i):
+        _, start, size = chunks[i]
         return pltpu.make_async_copy(
-            stage.at[i % n_stage, x_part],
-            parts_ref.at[
-                x_part, pl.ds(pl.multiple_of(shard * list_len, list_len), list_len)
-            ],
+            stage.at[i % n_stage, x_part, pl.ds(0, size)],
+            parts_ref.at[x_part, pl.ds(start, size)],
             x_local.at[i],
         )
 
-    def finish(i, offset):
+    def finish(i):
         for off in range(1, n_parts):
-            x_copy(i, offset, off).wait_send()
-        keep_copy(i, offset).wait()
+            x_copy(i, off).wait_send()
+        keep_copy(i).wait()
 
     lanes = [(0, 0), (1, 1), (0, 1), (1, 0)]
     loads[0].wait()
@@ -414,51 +454,61 @@
     loads[1].wait()
     turned.wait()
 
-    done = []
-    cells = {}
-
-    def weight_grads(offset, cell):
-        i = len(done)
-        shard = ring.at(offset)
-        for piece in range(2):
-            pair_copy(offset, piece).wait_recv()
-        cols = pl.ds(pl.multiple_of(shard * cols_dev, cols_dev), cols_dev)
-        fills = [
-            pltpu.make_async_copy(gall.at[side, cols], gw.at[cell, side], work_sem.at[side])
-            for side in range(2)
-        ]
+    offsets = [0]
+    for hop in range(1, half):
+        offsets += [-hop, hop]
+    offsets.append(half)
+
+    def cell_of(offset):
+        return offsets.index(offset) % cells * cols_dev
+
+    def weight_grads(step):
+        landed = [offset for offset in offsets if abs(offset) == step]
+        fills = []
+        for number, offset in enumerate(landed):
+            for piece in range(2):
+                pair_copy(offset, piece).wait_recv()
+            cols = pl.ds(pl.multiple_of(ring.at(offset) * cols_dev, cols_dev), cols_dev)
+            fills += [
+                pltpu.make_async_copy(
+                    gall.at[side, cols],
+                    gw.at[side, pl.ds(cell_of(offset), cols_dev)],
+                    work_sem.at[number, side],
+                )
+                for side in range(2)
+            ]
         for fill in fills:
             fill.start()
-        if i >= n_stage:
-            finish(i - n_stage, done[i - n_stage])
         for fill in fills:
             fill.wait()
-        slot = i % n_stage
-
-        def outer(j):
-            at = shard * list_len + j
-            r, c = row_tab[at], col_tab[at]
-            value = jnp.dot(
-                xt[0, r], gw[cell, 0, c], preferred_element_type=jnp.float32
-            ) + jnp.dot(xt[1, r], gw[cell, 1, c], preferred_element_type=jnp.float32)
-            for k in range(n_parts):
-                stage[slot, k, j] = value[k * band : (k + 1) * band].astype(jnp.bfloat16)
-
-        unrolled(list_len, outer)
-        for off in range(1, n_parts):
-            x_copy(i, offset, off).start()
-        keep_copy(i, offset).start()
-        done.append(offset)
-        cells[offset] = cell
+        for i, (at_step, start, size) in enumerate(chunks):
+            if at_step != step:
+                continue
+            if i >= n_stage:
+                finish(i - n_stage)
+            slot = i % n_stage
+
+            def outer(j):
+                r, block = list_row[start + j], list_block[start + j]
+                value = jnp.dot(
+                    xt[0, r], gw[0, block], preferred_element_type=jnp.float32
+                ) + jnp.dot(xt[1, r], gw[1, block], preferred_element_type=jnp.float32)
+                for k in range(n_parts):
+                    stage[slot, k, j] = value[k * band : (k + 1) * band].astype(jnp.bfloat16)
+
+            unrolled(size, outer)
+            for off in range(1, n_parts):
+                x_copy(i, off).start()
+            keep_copy(i).start()
 
     def token_grads(offset):
         shard = ring.at(offset)
-        cell = cells[offset]
+        cell = cell_of(offset)
 
         def back(j):
             at = shard * list_len + j
             term = lax.dot_general(
-                gw[cell, 0, col_tab[at]], ww[slot_tab[at]], (((1,), (1,)), ((), ())),
+                gw[0, cell + col_tab[at]], ww[slot_tab[at]], (((1,), (1,)), ((), ())),
                 preferred_element_type=jnp.float32,
             )
             buf[j + 1] = term + jnp.where(keep_tab[at] > 0, buf[j], 0.0)
@@ -478,7 +528,7 @@
             grad_copy(way, piece, hop + 1).start()
         pair_copy(-step_of(way) * (hop + 1), piece).start()
 
-    weight_grads(0, 0)
+    weight_grads(0)
     loads[2].wait()
     loads[3].wait()
     token_grads(0)
@@ -486,7 +536,7 @@
         arrive(0, 0, hop)
         arrive(1, 1, hop)
         if hop == half - 1:
-            weight_grads(half, 2)
+            weight_grads(half)
         if hop > 0:
             token_grads(-hop)
             token_grads(hop)
@@ -495,8 +545,7 @@
         else:
             arrive(0, 1, hop)
             arrive(1, 0, hop)
-            weight_grads(-hop - 1, 0)
-            weight_grads(hop + 1, 1)
+            weight_grads(hop + 1)
 
     def sum_copy(way, piece, hop):
         return pltpu.make_async_remote_copy(
@@ -537,23 +586,24 @@
             + recv[1, piece, half - 1].astype(jnp.float32)
         ).astype(jnp.bfloat16)
 
-    for i in range(max(0, n - n_stage), n):
-        finish(i, done[i])
-    for i in range(n):
+    for i in range(max(0, len(chunks) - n_stage), len(chunks)):
+        finish(i)
+    for i in range(len(chunks)):
         for off in range(1, n_parts):
-            x_copy(i, done[i], off).wait_recv()
+            x_copy(i, off).wait_recv()
     for way, piece in lanes:
         for hop in range(hops(ring, way, piece)):
             grad_copy(way, piece, hop).wait_send()
         for hop in range(first_hop(way, piece), half):
             sum_copy(way, piece, hop).wait_send()
-    for offset in done:
+    for offset in offsets:
         for piece in range(2):
             pair_copy(offset, piece).wait_send()
 
 
-def backward(tables, grads, xt, weights, n, list_len, rows, dp_size):
-    slot_tab, row_tab, col_tab, keep_tab, last_tab, _ = tables
+def backward(tables, listed, grads, xt, weights, n, list_len, rows, dp_size):
+    slot_tab, _, col_tab, keep_tab, last_tab, _ = tables
+    list_row, list_block, _ = listed
     _, tile_rows, half_tile, tokens = xt.shape
     cols_dev, _, pair = grads.shape
     tile = pair // 2
@@ -562,6 +612,8 @@
     band = tile // dp_size
     n_parts = dp_size // CORES
     n_stage = 4
+    chunks, cells = plan = arrival_plan(n, owned)
+    largest = max(size for _, _, size in chunks)
     dims = (n, tile_rows, cols_dev, list_len, rows, tokens, tile, dp_size)
     smem = pl.BlockSpec(memory_space=pltpu.SMEM)
     hbm = pl.BlockSpec(memory_space=pl.ANY)
@@ -573,7 +625,7 @@
     out_specs = [vmem, hbm]
     out_shape = [
         jax.ShapeDtypeStruct((tile_rows, rows, tile), jnp.bfloat16),
-        jax.ShapeDtypeStruct((n_parts, n * list_len, band, pair), jnp.bfloat16),
+        jax.ShapeDtypeStruct((n_parts, owned, band, pair), jnp.bfloat16),
     ]
     scratch = []
     if big:
@@ -582,55 +634,63 @@
     else:
         scratch.append(pltpu.VMEM(gall_shape, jnp.bfloat16))
     scratch += [
-        pltpu.VMEM((3, 2, cols_dev, tokens, pair), jnp.bfloat16),
+        pltpu.VMEM((2, cells * cols_dev, tokens, pair), jnp.bfloat16),
         pltpu.VMEM((owned, tile, pair), jnp.bfloat16),
         pltpu.VMEM((2, tile_rows, half_tile, tokens), jnp.bfloat16),
         pltpu.VMEM((list_len + 1, tokens, tile), jnp.float32),
         pltpu.VMEM((tile_rows, tokens, tile), jnp.float32),
-        pltpu.VMEM((n_stage, n_parts, list_len, band, pair), jnp.bfloat16),
+        pltpu.VMEM((n_stage, n_parts, largest, band, pair), jnp.bfloat16),
         pltpu.VMEM(slots, jnp.bfloat16),
         pltpu.VMEM(slots, jnp.bfloat16),
-        sem((4,)), sem((2,)),
+        sem((4,)), sem((2, 2)),
         sem((2, 2, half)), sem((2, 2, half)),
         sem((n, 2)), sem((n, 2)), sem((2,)),
-        sem((n, n_parts - 1)), sem((n, n_parts - 1)), sem((n,)),
+        sem((len(chunks), n_parts - 1)), sem((len(chunks), n_parts - 1)), sem((len(chunks),)),
         sem((2, 2, half)), sem((2, 2, half)),
     ]
     results = pl.pallas_call(
-        functools.partial(backward_kernel, dims, big),
+        functools.partial(backward_kernel, dims, plan),
         name="backward",
-        in_specs=[smem] * 5 + [hbm] * 3,
+        in_specs=[smem] * 6 + [hbm] * 3,
         out_specs=out_specs,
         out_shape=out_shape,
         scratch_shapes=scratch,
         compiler_params=pltpu.CompilerParams(
             collective_id=1, has_side_effects=True, vmem_limit_bytes=VMEM_LIMIT
         ),
-    )(slot_tab, row_tab, col_tab, keep_tab, last_tab, grads, xt, weights)
+    )(slot_tab, col_tab, keep_tab, last_tab, list_row, list_block, grads, xt, weights)
     return results[0], results[1]
 
 
-def finish_kernel(place_ref, parts_ref, out_ref):
+def finish_kernel(place_ref, parts_ref, d_ref, hidden_ref, out_ref, d_out, hidden_out):
     n_parts = parts_ref.shape[0]
     _, chunk, _, tile = out_ref.shape
     base = pl.program_id(0) * chunk
 
-    def one(p, carry):
+    @pl.when(pl.program_id(0) == 0)
+    def _():
+        for r in range(d_ref.shape[0]):
+            d_out[:, r * tile : (r + 1) * tile] = d_ref[r]
+
+    hidden_out[...] = hidden_ref[...]
+
+    def one(p):
         at = place_ref[base + p]
         total = parts_ref[0, at].astype(jnp.float32)
         for k in range(1, n_parts):
             total = total + parts_ref[k, at].astype(jnp.float32)
         out_ref[0, p] = total[:, :tile]
         out_ref[1, p] = total[:, tile:]
-        return carry
-
-    lax.fori_loop(0, chunk, one, 0)
-
-
-def finish_sum(place, parts):
+
+    unrolled(chunk, one)
+
+
+def finish_sum(place, parts, d, hidden):
     owned = place.shape[0]
     n_parts, listed, band, pair = parts.shape
     tile = pair // 2
+    tile_rows, rows, _ = d.shape
+    tokens, cols = hidden.shape
     steps = 8
     return pl.pallas_call(
         finish_kernel,
@@ -639,11 +699,21 @@
         in_specs=[
             pl.BlockSpec(memory_space=pltpu.SMEM),
             pl.BlockSpec((n_parts, listed, band, pair), lambda i: (0, 0, 0, 0)),
+            pl.BlockSpec((tile_rows, rows, tile), lambda i: (0, 0, 0)),
+            pl.BlockSpec((tokens // steps, cols), lambda i: (i, 0)),
         ],
-        out_specs=pl.BlockSpec((2, owned // steps, band, tile), lambda i: (0, i, 0, 0)),
-        out_shape=jax.ShapeDtypeStruct((2, owned, band, tile), jnp.float32),
+        out_specs=[
+            pl.BlockSpec((2, owned // steps, band, tile), lambda i: (0, i, 0, 0)),
+            pl.BlockSpec((rows, tile_rows * tile), lambda i: (0, 0)),
+            pl.BlockSpec((tokens // steps, cols), lambda i: (i, 0)),
+        ],
+        out_shape=[
+            jax.ShapeDtypeStruct((2, owned, band, tile), jnp.float32),
+            jax.ShapeDtypeStruct((rows, tile_rows * tile), d.dtype),
+            jax.ShapeDtypeStruct(hidden.shape, hidden.dtype),
+        ],
         compiler_params=pltpu.CompilerParams(vmem_limit_bytes=VMEM_LIMIT),
-    )(place, parts)
+    )(place, parts, d, hidden)
 
 
 def local(normed, cotangent, weight_tiles, slot_tile):
@@ -656,12 +726,12 @@
     tile_cols = cotangent.shape[1] // tile * n
     base_count = owned // n
     list_len = base_count + base_count // 4
-    by_col, by_row = build_tables(slot_tile, me, owned, tile_rows, tile_cols, n, list_len)
-    x = normed.reshape(rows, tile_rows, tile).transpose(1, 0, 2)
-    hidden, grads, xt = forward(by_col, x, cotangent, weight_tiles, n, list_len, dp_size)
-    d, parts = backward(by_row, grads, xt, weight_tiles, n, list_len, rows, dp_size)
-    grad_tiles = finish_sum(by_row[-1], parts)
-    d_normed = d.transpose(1, 0, 2).reshape(rows, width)
+    by_col, by_row, listed = build_tables(
+        slot_tile, me, owned, tile_rows, tile_cols, n, list_len
+    )
+    hidden, grads, xt = forward(by_col, normed, cotangent, weight_tiles, n, list_len, dp_size)
+    d, parts = backward(by_row, listed, grads, xt, weight_tiles, n, list_len, rows, dp_size)
+    grad_tiles, d_normed, hidden = finish_sum(listed[-1], parts, d, hidden)
     return hidden, d_normed, grad_tiles
 
 

time: 266 us -> 254 us (0.955)
  Pallas kernels: 256 us -> 247 us
  local copies, waits for them, and re-layouts: 5.24 us -> 0.01 us
    pallas_call x1, Pallas kernels: 133 us -> 122 us  [backward(): pl.pallas_call(functools.partial(backward_kernel, dims, plan), name='back...]
where the time goes in v3:
time: 254 us; the launch traced here: 253 us
  Pallas kernels  247 us (97%)
  other arithmetic  5.82 us (2%)
    pallas_call x1, Pallas kernels, backward(): pl.pallas_call(functools.partial(backward_kernel, dims, plan), name='back...  122 us
    pallas_call x1, Pallas kernels, forward(): pl.pallas_call(functools.partial(forward_kernel, dims), name='forward', i...  115 us
    pallas_call x1, Pallas kernels, finish_sum(): pl.pallas_call(finish_kernel, name='finish', grid=(steps,), in_specs=[pl....  9.23 us

profile of v3, /device:TPU:0, one launch (start us, length us, event | category | flops | bytes accessed | tf_op | source)
XLA Modules:
  0.0 253.2 jit_solution(8069958833729191457)
XLA Ops:
  0.7 0.8 multiply_add_fusion
  1.5 0.8 multiply_add_fusion.2
  2.2 0.3 convert_reduce_fusion
  2.5 0.1 broadcast_add_fusion.2
  2.6 0.7 select_reduce_fusion.9.last_tab
  3.3 0.2 convert_reduce_fusion.2.place_ref
  3.5 0.0 copy-start
  3.5 0.7 select_reduce_fusion.6
  4.2 0.0 copy-done
  4.2 1.0 select_reduce_fusion
  5.2 0.7 and_convert_fusion.1.keep_tab
  5.9 0.7 and_convert_fusion.keep_tab
  6.5 115.3 %forward.1 = (bf16[256,1024]{1,0:T(8,128)(2,1)}, bf16[8,256,256]{2,1,0:T(8,128)(2,1)}, bf16[2,32,64,256]{3,2,1,0:T(8,128)(2,1)}) custom-call(s32[320]{0:T(512)} %get-tuple-element.21.slot_tab, s32[320]{0:T(512)} %get-tuple-element.20.row_tab, s32[320]{0:T(512)} %and_convert_fusion.keep_tab, s32[64]{0:T(128)} %select_reduce_fusion.9.last_tab, ...), custom_call_target="tpu_custom_call" | custom-call | tf_op jit(solution)/shard_map/forward/pallas_call | solution.py:315
  121.9 122.2 %backward.1 = (bf16[32,32,128]{2,1,0:T(8,128)(2,1)}, bf16[2,256,32,256]{3,2,1,0:T(8,128)(2,1)}) custom-call(s32[320]{0:T(512)} %get-tuple-element.48.slot_tab, s32[320]{0:T(512)} %get-tuple-element.49.col_tab, s32[320]{0:T(512)} %and_convert_fusion.1.keep_tab, s32[256]{0:T(256)} %get-tuple-element.47.last_tab, s32[256]{0:T(256)} %get-tuple-element.25.list_row, ...), custom_call_target="tpu_custom_call" | custom-call | tf_op jit(solution)/shard_map/backward/pallas_call | solution.py:651
  244.0 9.2 %finish.1 = (f32[2,256,32,128]{3,2,1,0:T(8,128)}, bf16[32,4096]{1,0:T(8,128)(2,1)}, bf16[256,1024]{1,0:T(8,128)(2,1)}) custom-call(s32[256]{0:T(256)} %copy-done, bf16[2,256,32,256]{3,2,1,0:T(8,128)(2,1)} %get-tuple-element.13.parts_ref, bf16[32,32,128]{2,1,0:T(8,128)(2,1)} %get-tuple-element.14.d_ref, bf16[256,1024]{1,0:T(8,128)(2,1)} %get-tuple-element.15.hidden_ref), custom_call_target="tpu_custom_call" | custom-call | tf_op jit(solution)/shard_map/finish/pallas_call | solution.py:695
  (2 shorter events, 0.0 us)
Async XLA Ops:
  3.5 0.7 copy-start

commit v4 on v3

v4 whole, which is shorter than its diff:
```python
import functools

import jax
import jax.numpy as jnp
from jax import lax
from jax.experimental import pallas as pl
from jax.experimental.pallas import tpu as pltpu
from jax.sharding import PartitionSpec as P

MESH = pl.DeviceIdType.MESH
VMEM_LIMIT = 67_043_328
CORES = 2
FINE = 4


def ring_width(n):
    width = 2
    while 4 * width * width <= n:
        width *= 2
    return width


def split(value, by):
    if getattr(value, "ndim", 0) and by & (by - 1) == 0:
        return value >> (by.bit_length() - 1), value & (by - 1)
    return value // by, value % by


def ring_pos(index, n):
    y_size = ring_width(n)
    z, y = split(index, y_size)
    inner, _ = split(y + y_size - 1, y_size)
    _, odd = split(z, 2)
    snake = z * (y_size - 1) + (1 - odd) * (y - 1) + odd * (y_size - 1 - y)
    return inner * snake + (1 - inner) * (n - 1 - z)


def ring_index(pos, n):
    y_size = ring_width(n)
    z_size = n // y_size
    back = lax.div(pos, n - z_size)
    z = lax.div(pos, y_size - 1)
    k = lax.rem(pos, y_size - 1)
    odd = lax.rem(z, 2)
    y = (1 - odd) * (k + 1) + odd * (y_size - 1 - k)
    return (1 - back) * (z * y_size + y) + back * (n - 1 - pos) * y_size


def arrival(index, me, n):
    offset = ring_pos(index, n) - ring_pos(me, n)
    offset = jnp.where(offset < 0, offset + n, offset)
    behind = 2 * (n - offset) - 1
    return jnp.where(offset == 0, 0, jnp.where(offset < n // 2, 2 * offset, behind))


def arrival_plan(n, owned):
    base = owned // n
    low, high = base - base // 4, base + base // 4
    chunks, cells, start = [], 4, 0
    for step in range(n // 2 + 1):
        landed = min(2 * step + 1, n)
        stop = max(low * landed, owned - high * (n - landed))
        cells = max(cells, landed - start // high)
        sizes = []
        left = stop - start
        if left > 16:
            sizes.append(8)
            left -= 8
        if left > high:
            sizes.append(left // 8 * 4)
            left -= sizes[-1]
        sizes.append(left)
        for size in sizes:
            chunks.append((step, start, size))
            start += size
    return chunks, cells


class Ring:
    def __init__(self, n):
        self.n = n
        self.half = n // 2
        self.pos = ring_pos(lax.axis_index("tp"), n)

    def at(self, offset):
        return ring_index(lax.rem(self.pos + offset + self.n, self.n), self.n)


def hops(ring, way, piece):
    return ring.half if way == piece else ring.half - 1


def fine_hops(ring, way, quarter):
    return hops(ring, way, quarter // (FINE // 2))


def step_of(way):
    return 1 - 2 * way


def unrolled(count, body):
    by = max(size for size in range(1, 11) if count % size == 0)

    def steps(i, carry):
        for u in range(by):
            body(i * by + u)
        return carry

    lax.fori_loop(0, count // by, steps, 0)


SLOT_F, ROW_F, KEEP_F, LAST_F, SLOT_B, COL_B, KEEP_B, LAST_B, LIST_ROW, LIST_BLOCK = range(10)
GROUP, COL, ROW, KEY_F, KEY_B, KEY_A, SLOT, BLOCK = range(8)


def tile_fields(mine, me, tile_rows, tile_cols, n):
    owned = mine.shape[1]
    cols_dev = tile_cols // n
    row, col = split(mine, tile_cols)
    group, local_col = split(col, cols_dev)
    slots = lax.broadcasted_iota(jnp.int32, mine.shape, 1)
    order = arrival(group, me, n)
    _, cells = arrival_plan(n, owned)
    cell = order
    for _ in range(n // cells + 1):
        cell = jnp.where(cell >= cells, cell - cells, cell)
    return [
        group, local_col, row, col * tile_rows + row, row * tile_cols + col,
        order * owned + slots, slots, cell * cols_dev + local_col,
    ]


def write_tables(dims, me, slot_ref, by_row, tables, rank_ref):
    n, tile_rows, cols_dev, list_len, owned = dims
    mine = slot_ref[:, pl.ds(pl.multiple_of(me * owned, owned), owned)]
    for at, field in enumerate(tile_fields(mine, me, tile_rows, cols_dev * n, n)):
        by_row[at : at + 1, :] = field
    by_col = by_row[...].T

    def across(field):
        return by_row[field : field + 1, :]

    def down(field):
        return by_col[:, field : field + 1]

    def line(count):
        return lax.broadcasted_iota(jnp.int32, (owned, count), 1)

    def put(at, values):
        tables[at : at + 1, : values.shape[1]] = values

    def pick(hit, values):
        return jnp.sum(jnp.where(hit, values, 0), axis=0, keepdims=True)

    same = across(GROUP) == down(GROUP)

    def build(key, sub, n_sub, slot_at, field, field_at, most, keep_at, last_at):
        less = same & (across(key) < down(key))
        pos = jnp.sum(jnp.where(less, 1, 0), axis=1, keepdims=True)
        alike = less & (across(sub) == down(sub))
        keep = jnp.minimum(jnp.sum(jnp.where(alike, 1, 0), axis=1, keepdims=True), 1)
        hit = line(n * list_len) == down(GROUP) * list_len + pos
        put(slot_at, jnp.minimum(pick(hit, down(SLOT)), owned - 1))
        put(field_at, jnp.minimum(pick(hit, down(field)), most))
        put(keep_at, pick(hit, keep))
        inside = line(n * n_sub) == down(GROUP) * n_sub + down(sub)
        last = jnp.max(jnp.where(inside, pos + 1, 0), axis=0, keepdims=True)
        put(last_at, jnp.minimum(last, list_len))

    tables[...] = jnp.zeros(tables.shape, jnp.int32)
    build(KEY_F, COL, cols_dev, SLOT_F, ROW, ROW_F, tile_rows - 1, KEEP_F, LAST_F)
    build(KEY_B, ROW, tile_rows, SLOT_B, COL, COL_B, cols_dev - 1, KEEP_B, LAST_B)
    ahead = across(KEY_A) < down(KEY_A)
    rank = jnp.sum(jnp.where(ahead, 1, 0), axis=1, keepdims=True)
    hit = line(owned) == rank
    _, cells = arrival_plan(n, owned)
    put(LIST_ROW, jnp.minimum(pick(hit, down(ROW)), tile_rows - 1))
    put(LIST_BLOCK, jnp.minimum(pick(hit, down(BLOCK)), cells * cols_dev - 1))
    behind = down(KEY_A) < across(KEY_A)
    rank_ref[...] = jnp.sum(jnp.where(behind, 1, 0), axis=0, keepdims=True)


def step_kernel(dims, plan, big, slot_ref, x_ref, cot_ref, w_ref, *refs):
    n, tile_rows, cols_dev, list_len, rows, tokens, tile, dp_size, owned = dims
    hidden_ref, d_ref, parts_ref, rank_ref, mate, gall = refs[:6]
    (own, xg, ww, buf, acc, send, blocks, xt, stage, dsend, drecv, cot, hid,
     by_row, tables_v, tables,
     x_sem, load_sem, tab_sem, ag_send, ag_recv, rs_send, rs_recv,
     work_sem, g_send, g_recv, p_send, p_recv, t_sem,
     xs_send, xs_recv, x_local, ds_send, ds_recv) = refs[6:]
    ring = Ring(n)
    half = ring.half
    me = lax.axis_index("tp")
    me_dp = lax.axis_index("dp")
    core, x_part = lax.rem(me_dp, CORES), lax.div(me_dp, CORES)
    n_parts = dp_size // CORES
    band = tile // dp_size
    piece_cols = cols_dev // 2
    fine_rows = tile_rows // FINE
    n_stage = stage.shape[0]
    chunks, cells = plan
    partner = {"dp": x_part * CORES + 1 - core}
    seg = buf.shape[0] - 1
    n_seg = list_len // seg
    lower, upper = slice(0, tile), slice(tile, 2 * tile)

    own_rows = pl.ds(pl.multiple_of(me * rows, rows), rows)
    x_loads = [
        pltpu.make_async_copy(
            x_ref.at[:, pl.ds(r * tile, tile)], xg.at[r, own_rows, :], x_sem.at[r]
        )
        for r in range(tile_rows)
    ]
    loads = [
        pltpu.make_async_copy(cot_ref, cot, load_sem.at[0]),
        pltpu.make_async_copy(w_ref.at[0], ww.at[:, :, pl.ds(0, tile)], load_sem.at[1]),
        pltpu.make_async_copy(w_ref.at[1], ww.at[:, :, pl.ds(tile, tile)], load_sem.at[2]),
    ]
    for load in x_loads + loads:
        load.start()

    def x_device(off):
        return {"dp": lax.rem(x_part + off, n_parts) * CORES + core}

    barrier = pltpu.get_barrier_semaphore()
    for offset in (1, -1):
        pl.semaphore_signal(
            barrier, inc=1, device_id={"tp": ring.at(offset)}, device_id_type=MESH
        )
    pl.semaphore_signal(barrier, inc=1, device_id=partner, device_id_type=MESH)
    for off in range(1, n_parts):
        pl.semaphore_signal(barrier, inc=1, device_id=x_device(off), device_id_type=MESH)
    pl.semaphore_wait(barrier, 3 + n_parts - 1)
    for load in x_loads:
        load.wait()

    def token_copy(way, piece, hop):
        shard = ring.at(-step_of(way) * hop)
        view = xg.at[
            pl.ds(piece * fine_rows, fine_rows),
            pl.ds(pl.multiple_of(shard * rows, rows), rows),
            :,
        ]
        return pltpu.make_async_remote_copy(
            src_ref=view, dst_ref=view,
            send_sem=ag_send.at[way, piece, hop], recv_sem=ag_recv.at[way, piece, hop],
            device_id={"tp": ring.at(step_of(way))}, device_id_type=MESH,
        )

    lanes = [(0, 0), (1, 1), (0, 1), (1, 0)]
    fine_lanes = []
    for q in range(FINE):
        fine_lanes += [(0, q), (1, FINE - 1 - q)]
    for way, piece in fine_lanes:
        token_copy(way, piece, 0).start()
    write_tables(
        (n, tile_rows, cols_dev, list_len, owned), me, slot_ref, by_row, tables_v, rank_ref
    )
    for hop in range(half):
        for way, piece in fine_lanes:
            if hop < fine_hops(ring, way, piece):
                token_copy(way, piece, hop).wait_recv()
                if hop + 1 < fine_hops(ring, way, piece):
                    token_copy(way, piece, hop + 1).start()
        if hop == 0:
            table_copy = pltpu.make_async_copy(tables_v, tables, tab_sem.at[0])
            table_copy.start()
    table_copy.wait()
    loads[1].wait()
    loads[2].wait()

    def part_at(which, c, m):
        return (which * cols_dev + c) * 2 + m

    def compute(which, dest):
        buf[0] = jnp.zeros(buf.shape[1:], buf.dtype)
        for s in range(n_seg):
            if s > 0:
                buf[0] = buf[seg]

            def tile_step(j):
                at = dest * list_len + s * seg + j
                term = jnp.dot(
                    xg[tables[ROW_F, at]], ww[tables[SLOT_F, at]],
                    preferred_element_type=jnp.float32,
                )
                buf[j + 1] = term + jnp.where(tables[KEEP_F, at] > 0, buf[j], 0.0)

            unrolled(seg, tile_step)

            def column(c, carry):
                last = tables[LAST_F, dest * cols_dev + c]
                value = buf[jnp.clip(last - s * seg, 0, seg)]
                for m, side in enumerate((lower, upper)):
                    new = value[:, side]
                    if s > 0:
                        new = jnp.where(last > s * seg, new, acc[part_at(which, c, m)])
                    acc[part_at(which, c, m)] = new
                return carry

            lax.fori_loop(0, cols_dev, column, 0)

    def landing(way, piece, hop):
        return ((way * 2 + piece) * half + hop) * piece_cols

    def sum_copy(way, piece, hop):
        return pltpu.make_async_remote_copy(
            src_ref=send.at[way, piece, hop % 2],
            dst_ref=blocks.at[pl.ds(landing(way, piece, hop), piece_cols)],
            send_sem=rs_send.at[way, piece, hop], recv_sem=rs_recv.at[way, piece, hop],
            device_id={"tp": ring.at(step_of(way))}, device_id_type=MESH,
        )

    def first_hop(way, piece):
        return half - hops(ring, way, piece)

    def push(which, way, piece, hop):
        fresh = hop == first_hop(way, piece)
        if hop - 2 >= first_hop(way, piece):
            sum_copy(way, piece, hop - 2).wait_send()
        if not fresh:
            sum_copy(way, piece, hop - 1).wait_recv()

        def column(c, carry):
            for m, side in enumerate((lower, upper)):
                value = acc[part_at(which, piece * piece_cols + c, m)]
                if not fresh:
                    arrived = blocks[landing(way, piece, hop - 1) + c, :, side]
                    value = value + arrived.astype(jnp.float32)
                send[way, piece, hop % 2, c, :, side] = value.astype(jnp.bfloat16)
            return carry

        lax.fori_loop(0, piece_cols, column, 0)
        sum_copy(way, piece, hop).start()

    compute(0, ring.at(half))
    push(0, 0, 0, 0)
    push(0, 1, 1, 0)
    for hop in range(1, half):
        compute(0, ring.at(half - hop))
        compute(1, ring.at(hop - half))
        push(0, 0, 1, hop)
        push(1, 1, 0, hop)
        push(0, 0, 0, hop)
        push(1, 1, 1, hop)
    compute(0, me)

    order = lax.broadcasted_iota(jnp.int32, (tile, tile), 0)
    source = lax.broadcasted_iota(jnp.int32, (tile, tile), 1)
    for_core = (order // (n_parts * band) + core) % CORES
    for_part = order // band % n_parts
    perm = (source == (for_part * CORES + for_core) * band + order % band)
    perm = jnp.where(perm, 1.0, 0.0).astype(jnp.bfloat16)
    half_tile = tile // CORES

    def transpose_block(r):
        turned = lax.dot_general(
            perm, xg[r], (((1,), (1,)), ((), ())), preferred_element_type=jnp.float32
        ).astype(jnp.bfloat16)
        xt[0, r] = turned[:half_tile]
        xt[2, r] = turned[half_tile:]

    unrolled(tile_rows, transpose_block)
    turned_copy = pltpu.make_async_remote_copy(
        src_ref=xt.at[2], dst_ref=xt.at[1],
        send_sem=t_sem.at[0], recv_sem=t_sem.at[1],
        device_id=partner, device_id_type=MESH,
    )
    turned_copy.start()
    loads[0].wait()

    def piece_slice(shard, piece):
        start = pl.multiple_of(shard * cols_dev + piece * piece_cols, piece_cols)
        return pl.ds(start, piece_cols)

    def own_piece(piece):
        return own.at[pl.ds(piece * piece_cols, piece_cols)]

    def grad_copy(way, piece, hop):
        where = piece_slice(ring.at(-step_of(way) * hop), piece)
        return pltpu.make_async_remote_copy(
            src_ref=gall.at[where] if hop else own_piece(piece), dst_ref=gall.at[where],
            send_sem=g_send.at[way, piece, hop], recv_sem=g_recv.at[way, piece, hop],
            device_id={"tp": ring.at(step_of(way))}, device_id_type=MESH,
        )

    def pair_copy(offset, piece):
        where = piece_slice(ring.at(offset), piece)
        g = offset % n
        return pltpu.make_async_remote_copy(
            src_ref=gall.at[where] if offset else own_piece(piece), dst_ref=mate.at[where],
            send_sem=p_send.at[g, piece], recv_sem=p_recv.at[g, piece],
            device_id=partner, device_id_type=MESH,
        )

    def gate_piece(piece):
        for way in range(2):
            sum_copy(way, piece, half - 1).wait_recv()
        for k in range(piece_cols):
            c = piece * piece_cols + k
            gate, up = (
                acc[part_at(0, c, m)]
                + blocks[landing(0, piece, half - 1) + k, :, side].astype(jnp.float32)
                + blocks[landing(1, piece, half - 1) + k, :, side].astype(jnp.float32)
                for m, side in enumerate((lower, upper))
            )
            s = jax.nn.sigmoid(gate)
            act = gate * s
            columns = slice(c * tile, (c + 1) * tile)
            cotangent = cot[:, columns].astype(jnp.float32)
            hid[:, columns] = (act * up).astype(jnp.bfloat16)
            own[c, :, lower] = (
                cotangent * up * (s * (1.0 + gate * (1.0 - s)))
            ).astype(jnp.bfloat16)
            own[c, :, upper] = (cotangent * act).astype(jnp.bfloat16)

    gate_piece(0)
    grad_copy(0, 0, 0).start()
    gate_piece(1)
    for way, piece in lanes[1:]:
        grad_copy(way, piece, 0).start()
    for piece in range(2):
        pair_copy(0, piece).start()
    hidden_copy = pltpu.make_async_copy(hid, hidden_ref, load_sem.at[3])
    hidden_copy.start()

    def clear(r):
        acc[r] = jnp.zeros(acc.shape[1:], acc.dtype)

    unrolled(tile_rows, clear)
    turned_copy.wait()

    def x_copy(i, off):
        _, start, size = chunks[i]
        dest = lax.rem(x_part + off, n_parts)
        return pltpu.make_async_remote_copy(
            src_ref=stage.at[i % n_stage, dest, pl.ds(0, size)],
            dst_ref=parts_ref.at[x_part, pl.ds(start, size)],
            send_sem=xs_send.at[i, off - 1], recv_sem=xs_recv.at[i, off - 1],
            device_id=x_device(off), device_id_type=MESH,
        )

    def keep_copy(i):
        _, start, size = chunks[i]
        return pltpu.make_async_copy(
            stage.at[i % n_stage, x_part, pl.ds(0, size)],
            parts_ref.at[x_part, pl.ds(start, size)],
            x_local.at[i],
        )

    def finish(i):
        for off in range(1, n_parts):
            x_copy(i, off).wait_send()
        keep_copy(i).wait()

    offsets = [0]
    for hop in range(1, half):
        offsets += [-hop, hop]
    offsets.append(half)
    side_blocks = cells * cols_dev

    def cell_of(offset):
        return offsets.index(offset) % cells * cols_dev

    def landed(step):
        return [offset for offset in offsets if abs(offset) == step]

    def fill(step, side):
        copies = []
        for number, offset in enumerate(landed(step)):
            for piece in range(2):
                if side:
                    pair_copy(offset, piece).wait_recv()
                    ref = mate.at[piece_slice(ring.at(offset), piece)]
                elif offset:
                    ref = gall.at[piece_slice(ring.at(offset), piece)]
                else:
                    ref = own_piece(piece)
                first = side * side_blocks + cell_of(offset) + piece * piece_cols
                copies.append(
                    pltpu.make_async_copy(
                        ref, blocks.at[pl.ds(first, piece_cols)],
                        work_sem.at[number, side, piece],
                    )
                )
                copies[-1].start()
        return copies

    def settle(copies):
        for copy in copies:
            copy.wait()

    def weight_grads(step, which=None):
        at_this = [i for i, chunk in enumerate(chunks) if chunk[0] == step]
        for i in at_this if which is None else at_this[which : which + 1]:
            _, start, size = chunks[i]
            if i >= n_stage:
                finish(i - n_stage)
            slot = i % n_stage

            def outer(j):
                r, block = tables[LIST_ROW, start + j], tables[LIST_BLOCK, start + j]
                value = jnp.dot(
                    xt[0, r], blocks[block], preferred_element_type=jnp.float32
                ) + jnp.dot(
                    xt[1, r], blocks[side_blocks + block], preferred_element_type=jnp.float32
                )
                for k in range(n_parts):
                    stage[slot, k, j] = value[k * band : (k + 1) * band].astype(jnp.bfloat16)

            unrolled(size, outer)
            for off in range(1, n_parts):
                x_copy(i, off).start()
            keep_copy(i).start()

    def token_grads(offset, source=None):
        shard = ring.at(offset)
        source = blocks if source is None else source
        cell = cell_of(offset) if source is blocks else shard * cols_dev
        buf[0] = jnp.zeros(buf.shape[1:], buf.dtype)
        for s, side in zip(range(n_seg), (lower, upper)):
            if s > 0:
                buf[0, :, side] = buf[seg, :, lower]

            def back(j):
                at = shard * list_len + s * seg + j
                term = lax.dot_general(
                    source[cell + tables[COL_B, at]], ww[tables[SLOT_B, at]],
                    (((1,), (1,)), ((), ())), preferred_element_type=jnp.float32,
                )
                kept = jnp.where(tables[KEEP_B, at] > 0, buf[j, :, side], 0.0)
                buf[j + 1, :, side] = term + kept

            unrolled(seg, back)

        def add_row(r):
            last = tables[LAST_B, shard * tile_rows + r]
            value = buf[jnp.minimum(last, seg), :, lower]
            if n_seg > 1:
                later = buf[jnp.maximum(last - seg, 0), :, upper]
                value = jnp.where(last > seg, later, value)
            acc[r] += value

        unrolled(tile_rows, add_row)

    def arrive(way, piece, hop):
        if hop >= hops(ring, way, piece):
            return
        grad_copy(way, piece, hop).wait_recv()
        if hop + 1 < hops(ring, way, piece):
            grad_copy(way, piece, hop + 1).start()
        pair_copy(-step_of(way) * (hop + 1), piece).start()

    settle(fill(0, 0))
    settle(fill(0, 1))
    weight_grads(0)
    token_grads(0)
    for hop in range(half - 1):
        arrive(0, 0, hop)
        arrive(1, 1, hop)
        if hop > 0:
            token_grads(-hop)
            token_grads(hop)
        arrive(0, 1, hop)
        arrive(1, 0, hop)
        settle(fill(hop + 1, 0) + fill(hop + 1, 1))
        if hop < half - 2:
            weight_grads(hop + 1)
    last = half - 1
    n_last = len([chunk for chunk in chunks if chunk[0] == last])
    n_half = len([chunk for chunk in chunks if chunk[0] == half])
    weight_grads(last, 0)
    token_grads(-last)
    for which in range(1, n_last):
        weight_grads(last, which)
    token_grads(last)
    arrive(0, 0, last)
    arrive(1, 1, last)
    if big:
        settle(fill(half, 0))
        fills = []
        token_grads(half)
    else:
        fills = fill(half, 0)
        token_grads(half, gall)

    def d_copy(way, piece, hop):
        return pltpu.make_async_remote_copy(
            src_ref=dsend.at[way, piece, hop], dst_ref=drecv.at[way, piece, hop],
            send_sem=ds_send.at[way, piece, hop], recv_sem=ds_recv.at[way, piece, hop],
            device_id={"tp": ring.at(step_of(way))}, device_id_type=MESH,
        )

    def own_term(dest, piece):
        return acc[
            pl.ds(piece * fine_rows, fine_rows),
            pl.ds(pl.multiple_of(dest * rows, rows), rows),
            :,
        ]

    def d_first(way, piece):
        return half - fine_hops(ring, way, piece)

    def d_push(way, piece, hop):
        value = own_term(ring.at(step_of(way) * (half - hop)), piece)
        if hop > d_first(way, piece):
            d_copy(way, piece, hop - 1).wait_recv()
            value = value + drecv[way, piece, hop - 1].astype(jnp.float32)
        dsend[way, piece, hop] = value.astype(jnp.bfloat16)
        d_copy(way, piece, hop).start()

    for hop in range(half):
        fresh = [lane for lane in fine_lanes if hop == d_first(*lane)]
        going = [lane for lane in fine_lanes if hop > d_first(*lane)]
        for way, piece in fresh + going:
            d_push(way, piece, hop)
        if hop == 0:
            settle(fills + fill(half, 1))
        if hop < n_half:
            weight_grads(half, hop)
    for piece in range(FINE):
        for way in range(2):
            d_copy(way, piece, half - 1).wait_recv()
        d_ref[pl.ds(piece * fine_rows, fine_rows)] = (
            own_term(me, piece)
            + drecv[0, piece, half - 1].astype(jnp.float32)
            + drecv[1, piece, half - 1].astype(jnp.float32)
        ).astype(jnp.bfloat16)

    for i in range(max(0, len(chunks) - n_stage), len(chunks)):
        finish(i)
    for i in range(len(chunks)):
        for off in range(1, n_parts):
            x_copy(i, off).wait_recv()
    for way, piece in lanes:
        for hop in range(hops(ring, way, piece)):
            grad_copy(way, piece, hop).wait_send()
        for hop in range(max(first_hop(way, piece), half - 2), half):
            sum_copy(way, piece, hop).wait_send()
    for way, piece in fine_lanes:
        for hop in range(fine_hops(ring, way, piece)):
            token_copy(way, piece, hop).wait_send()
        for hop in range(d_first(way, piece), half):
            d_copy(way, piece, hop).wait_send()
    for offset in offsets:
        for piece in range(2):
            pair_copy(offset, piece).wait_send()
    hidden_copy.wait()


def step(slot_tile, normed, cotangent, weights, n, list_len, dp_size):
    rows, width = normed.shape
    owned, tile = weights.shape[1:3]
    tile_rows = width // tile
    tokens, cols = cotangent.shape
    cols_dev = cols // tile
    pair = 2 * tile
    half = n // 2
    band = tile // dp_size
    n_parts = dp_size // CORES
    n_stage = 4
    chunks, cells = plan = arrival_plan(n, owned)
    largest = max(size for _, _, size in chunks)
    dims = (n, tile_rows, cols_dev, list_len, rows, tokens, tile, dp_size, owned)
    hbm = pl.BlockSpec(memory_space=pl.ANY)
    vmem = pl.BlockSpec(memory_space=pltpu.VMEM)
    sem = pltpu.SemaphoreType.DMA
    gall_shape = (n * cols_dev, tokens, pair)
    big = n * cols_dev * tokens * pair * 2 > 12 * 2**20
    seg = list_len // 2 if list_len % 8 == 0 else list_len
    most = -(-max(n * list_len, n * tile_rows, owned) // tile) * tile
    d_slots = (2, FINE, half, tile_rows // FINE, rows, tile)
    out_specs = [hbm, vmem, hbm, vmem, hbm]
    out_shape = [
        jax.ShapeDtypeStruct((tokens, cols), jnp.bfloat16),
        jax.ShapeDtypeStruct((tile_rows, rows, tile), jnp.bfloat16),
        jax.ShapeDtypeStruct((n_parts, owned, band, pair), jnp.bfloat16),
        jax.ShapeDtypeStruct((1, owned), jnp.int32),
        jax.ShapeDtypeStruct(gall_shape, jnp.bfloat16),
    ]
    scratch = []
    if big:
        out_specs.append(hbm)
        out_shape.append(jax.ShapeDtypeStruct(gall_shape, jnp.bfloat16))
    else:
        scratch.append(pltpu.VMEM(gall_shape, jnp.bfloat16))
    n_blocks = max(4 * half * (cols_dev // 2), 2 * cells * cols_dev)
    scratch += [
        pltpu.VMEM((cols_dev, tokens, pair), jnp.bfloat16),
        pltpu.VMEM((tile_rows, tokens, tile), jnp.bfloat16),
        pltpu.VMEM((owned, tile, pair), jnp.bfloat16),
        pltpu.VMEM((seg + 1, tokens, pair), jnp.float32),
        pltpu.VMEM((max(4 * cols_dev, tile_rows), tokens, tile), jnp.float32),
        pltpu.VMEM((2, 2, 2, cols_dev // 2, tokens, pair), jnp.bfloat16),
        pltpu.VMEM((n_blocks, tokens, pair), jnp.bfloat16),
        pltpu.VMEM((3, tile_rows, tile // CORES, tokens), jnp.bfloat16),
        pltpu.VMEM((n_stage, n_parts, largest, band, pair), jnp.bfloat16),
        pltpu.VMEM(d_slots, jnp.bfloat16),
        pltpu.VMEM(d_slots, jnp.bfloat16),
        pltpu.VMEM((tokens, cols), jnp.bfloat16),
        pltpu.VMEM((tokens, cols), jnp.bfloat16),
        pltpu.VMEM((8, owned), jnp.int32),
        pltpu.VMEM((16, most), jnp.int32),
        pltpu.SMEM((16, most), jnp.int32),
        sem((tile_rows,)), sem((4,)), sem((1,)),
        sem((2, FINE, half)), sem((2, FINE, half)), sem((2, 2, half)), sem((2, 2, half)),
        sem((2, 2, 2)), sem((2, 2, half)), sem((2, 2, half)),
        sem((n, 2)), sem((n, 2)), sem((2,)),
        sem((len(chunks), n_parts - 1)), sem((len(chunks), n_parts - 1)), sem((len(chunks),)),
        sem((2, FINE, half)), sem((2, FINE, half)),
    ]
    results = pl.pallas_call(
        functools.partial(step_kernel, dims, plan, big),
        name="step",
        in_specs=[vmem, hbm, hbm, hbm],
        out_specs=out_specs,
        out_shape=out_shape,
        scratch_shapes=scratch,
        compiler_params=pltpu.CompilerParams(
            collective_id=0, has_side_effects=True, vmem_limit_bytes=VMEM_LIMIT
        ),
    )(slot_tile.reshape(1, -1), normed, cotangent, weights)
    return results[:4]


def finish_kernel(place_ref, parts_ref, d_ref, hidden_ref, out_ref, d_out, hidden_out):
    n_parts = parts_ref.shape[0]
    _, chunk, _, tile = out_ref.shape
    base = pl.program_id(0) * chunk

    @pl.when(pl.program_id(0) == 0)
    def _():
        for r in range(d_ref.shape[0]):
            d_out[:, r * tile : (r + 1) * tile] = d_ref[r]

    hidden_out[...] = hidden_ref[...]

    def one(p):
        at = place_ref[base + p]
        total = parts_ref[0, at].astype(jnp.float32)
        for k in range(1, n_parts):
            total = total + parts_ref[k, at].astype(jnp.float32)
        out_ref[0, p] = total[:, :tile]
        out_ref[1, p] = total[:, tile:]

    unrolled(chunk, one)


def finish_sum(place, parts, d, hidden):
    owned = place.shape[0]
    n_parts, listed, band, pair = parts.shape
    tile = pair // 2
    tile_rows, rows, _ = d.shape
    tokens, cols = hidden.shape
    steps = 2
    return pl.pallas_call(
        finish_kernel,
        name="finish",
        grid=(steps,),
        in_specs=[
            pl.BlockSpec(memory_space=pltpu.SMEM),
            pl.BlockSpec((n_parts, listed, band, pair), lambda i: (0, 0, 0, 0)),
            pl.BlockSpec((tile_rows, rows, tile), lambda i: (0, 0, 0)),
            pl.BlockSpec((tokens // steps, cols), lambda i: (i, 0)),
        ],
        out_specs=[
            pl.BlockSpec((2, owned // steps, band, tile), lambda i: (0, i, 0, 0)),
            pl.BlockSpec((rows, tile_rows * tile), lambda i: (0, 0)),
            pl.BlockSpec((tokens // steps, cols), lambda i: (i, 0)),
        ],
        out_shape=[
            jax.ShapeDtypeStruct((2, owned, band, tile), jnp.float32),
            jax.ShapeDtypeStruct((rows, tile_rows * tile), d.dtype),
            jax.ShapeDtypeStruct(hidden.shape, hidden.dtype),
        ],
        compiler_params=pltpu.CompilerParams(vmem_limit_bytes=VMEM_LIMIT),
    )(place, parts, d, hidden)


def local(normed, cotangent, weight_tiles, slot_tile):
    n = lax.axis_size("tp")
    dp_size = lax.axis_size("dp")
    owned = weight_tiles.shape[1]
    base_count = owned // n
    list_len = base_count + base_count // 4
    hidden, d, parts, rank = step(
        slot_tile, normed, cotangent, weight_tiles, n, list_len, dp_size
    )
    grad_tiles, d_normed, hidden = finish_sum(rank.reshape(owned), parts, d, hidden)
    return hidden, d_normed, grad_tiles


def solution(mesh):
    return jax.shard_map(
        local,
        mesh=mesh,
        in_specs=(P(("dp", "tp"), None), P("dp", "tp"), P(None, "tp", None, None), P()),
        out_specs=(P("dp", "tp"), P(("dp", "tp"), None), P(None, "tp", "dp", None)),
        check_vma=False,
    )
```

time: 254 us -> 240 us (0.945)
  Pallas kernels: 247 us -> 238 us
  other arithmetic: 5.82 us -> 0 us
    pallas_call x2 -> x1, Pallas kernels: 237 us -> 231 us  [step(): pl.pallas_call(functools.partial(step_kernel, dims, plan, big), name='ste...]
where the time goes in v4:
time: 240 us; the launch traced here: 239 us
  Pallas kernels  238 us (99%)
    pallas_call x1, Pallas kernels, step(): pl.pallas_call(functools.partial(step_kernel, dims, plan, big), name='ste...  231 us
    pallas_call x1, Pallas kernels, finish_sum(): pl.pallas_call(finish_kernel, name='finish', grid=(steps,), in_specs=[pl....  7.62 us

profile of v4, /device:TPU:0, one launch (start us, length us, event | category | flops | bytes accessed | tf_op | source)
XLA Modules:
  0.0 238.9 jit_solution(6765201885731915899)
XLA Ops:
  0.6 230.5 %step.1 = (bf16[256,1024]{1,0:T(8,128)(2,1)}, bf16[32,32,128]{2,1,0:T(8,128)(2,1)}, bf16[2,256,32,256]{3,2,1,0:T(8,128)(2,1)}, s32[1,256]{1,0:T(1,128)}, bf16[64,256,256]{2,1,0:T(8,128)(2,1)}) custom-call(s32[1,2048]{1,0:T(1,128)} %bitcast.2, bf16[32,4096]{1,0:T(8,128)(2,1)} %x_ref.1, bf16[256,1024]{1,0:T(8,128)(2,1)} %cot_ref.1, ...), custom_call_target="tpu_custom_call" | custom-call | tf_op jit(solution)/shard_map/step/pallas_call | solution.py:712
  231.2 7.6 %finish.1 = (f32[2,256,32,128]{3,2,1,0:T(8,128)}, bf16[32,4096]{1,0:T(8,128)(2,1)}, bf16[256,1024]{1,0:T(8,128)(2,1)}) custom-call(s32[256]{0:T(256)} %bitcast.3, bf16[2,256,32,256]{3,2,1,0:T(8,128)(2,1)} %get-tuple-element.11.parts_ref, bf16[32,32,128]{2,1,0:T(8,128)(2,1)} %get-tuple-element.12.d_ref, bf16[256,1024]{1,0:T(8,128)(2,1)} %get-tuple-element.13.hidden_ref), custom_call_target="tpu_custom_call" | custom-call | tf_op jit(solution)/shard_map/finish/pallas_call | solution.py:756

commit v5 on v4

--- a/solution.py
+++ b/solution.py
@@ -231,9 +231,6 @@
     for off in range(1, n_parts):
         pl.semaphore_signal(barrier, inc=1, device_id=x_device(off), device_id_type=MESH)
     pl.semaphore_wait(barrier, 3 + n_parts - 1)
-    for load in x_loads:
-        load.wait()
-
     def token_copy(way, piece, hop):
         shard = ring.at(-step_of(way) * hop)
         view = xg.at[
@@ -251,7 +248,12 @@
     fine_lanes = []
     for q in range(FINE):
         fine_lanes += [(0, q), (1, FINE - 1 - q)]
+    loaded = set()
     for way, piece in fine_lanes:
+        if piece not in loaded:
+            for load in x_loads[piece * fine_rows : (piece + 1) * fine_rows]:
+                load.wait()
+            loaded.add(piece)
         token_copy(way, piece, 0).start()
     write_tables(
         (n, tile_rows, cols_dev, list_len, owned), me, slot_ref, by_row, tables_v, rank_ref
@@ -569,10 +571,10 @@
     last = half - 1
     n_last = len([chunk for chunk in chunks if chunk[0] == last])
     n_half = len([chunk for chunk in chunks if chunk[0] == half])
-    weight_grads(last, 0)
+    for which in range(n_last - 1):
+        weight_grads(last, which)
     token_grads(-last)
-    for which in range(1, n_last):
-        weight_grads(last, which)
+    weight_grads(last, n_last - 1)
     token_grads(last)
     arrive(0, 0, last)
     arrive(1, 1, last)

time: 240 us -> 238 us (level)
  no operation moved by 1% of the time
where the time goes in v5:
time: 238 us
  Pallas kernels  237 us (100%)
    pallas_call x1, Pallas kernels, step(): pl.pallas_call(functools.partial(step_kernel, dims, plan, big), name='ste...  229 us
    pallas_call x1, Pallas kernels, finish_sum(): pl.pallas_call(finish_kernel, name='finish', grid=(steps,), in_specs=[pl....  7.62 us

profile of v5, /device:TPU:0, one launch (start us, length us, event | category | flops | bytes accessed | tf_op | source)
XLA Modules:
  0.0 237.8 jit_solution(9815030212314461330)
XLA Ops:
  0.6 229.4 %step.1 = (bf16[256,1024]{1,0:T(8,128)(2,1)}, bf16[32,32,128]{2,1,0:T(8,128)(2,1)}, bf16[2,256,32,256]{3,2,1,0:T(8,128)(2,1)}, s32[1,256]{1,0:T(1,128)}, bf16[64,256,256]{2,1,0:T(8,128)(2,1)}) custom-call(s32[1,2048]{1,0:T(1,128)} %bitcast.2, bf16[32,4096]{1,0:T(8,128)(2,1)} %x_ref.1, bf16[256,1024]{1,0:T(8,128)(2,1)} %cot_ref.1, ...), custom_call_target="tpu_custom_call" | custom-call | tf_op jit(solution)/shard_map/step/pallas_call | solution.py:714
  230.1 7.6 %finish.1 = (f32[2,256,32,128]{3,2,1,0:T(8,128)}, bf16[32,4096]{1,0:T(8,128)(2,1)}, bf16[256,1024]{1,0:T(8,128)(2,1)}) custom-call(s32[256]{0:T(256)} %bitcast.3, bf16[2,256,32,256]{3,2,1,0:T(8,128)(2,1)} %get-tuple-element.11.parts_ref, bf16[32,32,128]{2,1,0:T(8,128)(2,1)} %get-tuple-element.12.d_ref, bf16[256,1024]{1,0:T(8,128)(2,1)} %get-tuple-element.13.hidden_ref), custom_call_target="tpu_custom_call" | custom-call | tf_op jit(solution)/shard_map/finish/pallas_call | solution.py:758
